TPU v7x, 128 devices: a whole 4x4x4 slice. The times are simulated.
128 devices in a mesh: sys: 1, col: 2 (over core), seg: 64 (over z, y, x).
Axes of the slice: x: 4, y: 4, z: 4, core: 2. Of those that a mesh axis runs over, the one named last changes fastest.
Arguments:
- positions: bfloat16 [131072, 128], P(('sys', 'seg', 'col'))
- charges: float32 [131072], P(('sys', 'seg', 'col'))
Outputs:
- output 1: float32 [131072, 128], P(('sys', 'seg', 'col'))
- output 2: float32 [1], P('sys')
All inputs are finite; a program needn't handle non-finite values.
Results may differ from a plain program's by a relative error of at most 0.001.
Values are sent between devices in bfloat16 or wider.
A program may use at most 1 GiB of HBM per device.

v0:
```python
import jax
import jax.numpy as jnp
from jax import lax
from jax.sharding import PartitionSpec as P

ROW_AXES = ('sys', 'seg', 'col')


def pair_weights(x_host, q_host, sq_host, x_vis, q_vis, inv_len2):
    sq_vis = jnp.sum(jnp.square(x_vis.astype(jnp.float32)), axis=1)
    dot_prod = lax.dot_general(x_host, x_vis, (((1,), (1,)), ((), ())), preferred_element_type=jnp.float32)
    sq_dist = jnp.maximum(sq_host[:, None] + sq_vis[None, :] - 2.0 * dot_prod, 0.0)
    return q_host[:, None] * q_vis[None, :] * jnp.exp(-0.5 * inv_len2 * sq_dist)


def host_terms(weights, w_low, x_host, x_vis):
    pulled = jnp.dot(w_low, x_vis, preferred_element_type=jnp.float32)
    return jnp.sum(weights, axis=1)[:, None] * x_host.astype(jnp.float32) - pulled


def visitor_terms(weights, w_low, x_host, x_vis):
    pushed = lax.dot_general(w_low, x_host, (((0,), (0,)), ((), ())), preferred_element_type=jnp.float32)
    return jnp.sum(weights, axis=0)[:, None] * x_vis.astype(jnp.float32) - pushed


def solution(mesh):
    seg_size = mesh.shape['seg']
    col_size = mesh.shape['col']
    far_step = seg_size // 2
    full_steps = (seg_size - 1) // 2
    forward = [(source, (source + 1) % seg_size) for source in range(seg_size)]
    back_home = [(source, (source - far_step) % seg_size) for source in range(seg_size)]

    def per_device(x_own, q_own):
        own_rows, feat_dim = x_own.shape
        inv_len2 = 1.0 / feat_dim
        team_rows = own_rows * col_size
        own_pos = lax.axis_index('col') * own_rows + jnp.arange(own_rows)
        team_pos = jnp.arange(team_rows)
        sq_own = jnp.sum(jnp.square(x_own.astype(jnp.float32)), axis=1)
        x_team = lax.all_gather(x_own, 'col', axis=0, tiled=True)
        q_team = lax.all_gather(q_own, 'col', axis=0, tiled=True)

        weights = pair_weights(x_own, q_own, sq_own, x_team, q_team, inv_len2)
        weights = jnp.where(own_pos[:, None] == team_pos[None, :], 0.0, weights)
        own_force = host_terms(weights, weights.astype(jnp.bfloat16), x_own, x_team)
        energy = 0.5 * jnp.sum(weights)

        def visit(x_vis, q_vis, reaction, own_force, energy, masked):
            weights = pair_weights(x_own, q_own, sq_own, x_vis, q_vis, inv_len2)
            if masked:
                low_half = lax.axis_index('seg') < far_step
                host_keep = jnp.where(low_half | (own_pos >= team_rows // 2), 1.0, 0.0)
                vis_keep = jnp.where(low_half & (team_pos >= team_rows // 2), 0.0, 1.0)
                weights = weights * host_keep[:, None] * vis_keep[None, :]
            w_low = weights.astype(jnp.bfloat16)
            own_force = own_force + host_terms(weights, w_low, x_own, x_vis)
            reaction = reaction + visitor_terms(weights, w_low, x_own, x_vis)
            return reaction, own_force, energy + jnp.sum(weights)

        x_vis = lax.ppermute(x_team, 'seg', forward)
        q_vis = lax.ppermute(q_team, 'seg', forward)
        reaction = jnp.zeros((team_rows, feat_dim), jnp.float32)
        reaction, own_force, energy = visit(x_vis, q_vis, reaction, own_force, energy, full_steps == 0)

        def step_body(step_idx, loop_state):
            x_vis, q_vis, reaction, own_force, energy = loop_state
            x_vis = lax.ppermute(x_vis, 'seg', forward)
            q_vis = lax.ppermute(q_vis, 'seg', forward)
            reaction = lax.ppermute(reaction, 'seg', forward)
            reaction, own_force, energy = visit(x_vis, q_vis, reaction, own_force, energy, False)
            return x_vis, q_vis, reaction, own_force, energy

        loop_state = lax.fori_loop(1, full_steps, step_body, (x_vis, q_vis, reaction, own_force, energy))
        x_vis, q_vis, reaction, own_force, energy = loop_state
        if 0 < full_steps < far_step:
            x_vis = lax.ppermute(x_vis, 'seg', forward)
            q_vis = lax.ppermute(q_vis, 'seg', forward)
            reaction = lax.ppermute(reaction, 'seg', forward)
            reaction, own_force, energy = visit(x_vis, q_vis, reaction, own_force, energy, True)

        reaction = lax.psum_scatter(reaction, 'col', scatter_dimension=0, tiled=True)
        reaction = lax.ppermute(reaction, 'seg', back_home)
        energy = lax.psum(energy, ('seg', 'col'))
        return (own_force + reaction) * inv_len2, energy.reshape(1)

    row_spec = P(ROW_AXES, None)
    return jax.shard_map(per_device, mesh=mesh, in_specs=(row_spec, P(ROW_AXES)), out_specs=(row_spec, P('sys')), check_vma=False)
```

profile of v0, /device:TPU:1, one launch (start us, length us, event | category | flops | bytes accessed | tf_op | source)
XLA Modules:
  0.0 1342.3 jit_solution(17018618162896296238)
XLA Ops:
  44.1 1136.2 %while.18 = (s32[]{:T(128)}, bf16[2048,128]{1,0:T(8,128)(2,1)S(1)}, f32[2048]{0:T(1024)S(1)}, f32[2048,128]{1,0:T(8,128)}, f32[1024,128]{1,0:T(8,128)S(1)}, /*in...) while((s32[]{:T(128)}, bf16[2048,128]{1,0:T(8,128)(2,1)S(1)}, ...), condition=%wide.region_13.14_spmd, body=%wide.region_8.13_spmd.sunk | while | flops 1636035584 | bytes 42836232 | solution.py:74
  45.6 16.4 %collective-permute-done.1 = f32[2048]{0:T(1024)S(1)} collective-permute-done((f32[2048]{0:T(1024)S(1)}, f32[2048]{0:T(1024)S(1)}, u32[]{:S(2)}, u32[]{:S(2)}) %collective-permute-start.1) | collective-permute-done | bytes 8224 | tf_op jit(solution)/shard_map/while/body/eval_jaxpr/ppermute | solution.py:69
  86.9 16.3 %collective-permute-done.1 = f32[2048]{0:T(1024)S(1)} collective-permute-done((f32[2048]{0:T(1024)S(1)}, f32[2048]{0:T(1024)S(1)}, u32[]{:S(2)}, u32[]{:S(2)}) %collective-permute-start.1) | collective-permute-done | bytes 8224 | tf_op jit(solution)/shard_map/while/body/eval_jaxpr/ppermute | solution.py:69
  128.1 15.0 %collective-permute-done.1 = f32[2048]{0:T(1024)S(1)} collective-permute-done((f32[2048]{0:T(1024)S(1)}, f32[2048]{0:T(1024)S(1)}, u32[]{:S(2)}, u32[]{:S(2)}) %collective-permute-start.1) | collective-permute-done | bytes 8224 | tf_op jit(solution)/shard_map/while/body/eval_jaxpr/ppermute | solution.py:69
  168.0 13.5 %collective-permute-done.1 = f32[2048]{0:T(1024)S(1)} collective-permute-done((f32[2048]{0:T(1024)S(1)}, f32[2048]{0:T(1024)S(1)}, u32[]{:S(2)}, u32[]{:S(2)}) %collective-permute-start.1) | collective-permute-done | bytes 8224 | tf_op jit(solution)/shard_map/while/body/eval_jaxpr/ppermute | solution.py:69
  206.6 13.5 %collective-permute-done.1 = f32[2048]{0:T(1024)S(1)} collective-permute-done((f32[2048]{0:T(1024)S(1)}, f32[2048]{0:T(1024)S(1)}, u32[]{:S(2)}, u32[]{:S(2)}) %collective-permute-start.1) | collective-permute-done | bytes 8224 | tf_op jit(solution)/shard_map/while/body/eval_jaxpr/ppermute | solution.py:69
  243.9 13.5 %collective-permute-done.1 = f32[2048]{0:T(1024)S(1)} collective-permute-done((f32[2048]{0:T(1024)S(1)}, f32[2048]{0:T(1024)S(1)}, u32[]{:S(2)}, u32[]{:S(2)}) %collective-permute-start.1) | collective-permute-done | bytes 8224 | tf_op jit(solution)/shard_map/while/body/eval_jaxpr/ppermute | solution.py:69
  347.6 15.6 %collective-permute-done.1 = f32[2048]{0:T(1024)S(1)} collective-permute-done((f32[2048]{0:T(1024)S(1)}, f32[2048]{0:T(1024)S(1)}, u32[]{:S(2)}, u32[]{:S(2)}) %collective-permute-start.1) | collective-permute-done | bytes 8224 | tf_op jit(solution)/shard_map/while/body/eval_jaxpr/ppermute | solution.py:69
  382.2 16.3 %collective-permute-done.1 = f32[2048]{0:T(1024)S(1)} collective-permute-done((f32[2048]{0:T(1024)S(1)}, f32[2048]{0:T(1024)S(1)}, u32[]{:S(2)}, u32[]{:S(2)}) %collective-permute-start.1) | collective-permute-done | bytes 8224 | tf_op jit(solution)/shard_map/while/body/eval_jaxpr/ppermute | solution.py:69
  416.7 17.0 %collective-permute-done.1 = f32[2048]{0:T(1024)S(1)} collective-permute-done((f32[2048]{0:T(1024)S(1)}, f32[2048]{0:T(1024)S(1)}, u32[]{:S(2)}, u32[]{:S(2)}) %collective-permute-start.1) | collective-permute-done | bytes 8224 | tf_op jit(solution)/shard_map/while/body/eval_jaxpr/ppermute | solution.py:69
  451.2 17.8 %collective-permute-done.1 = f32[2048]{0:T(1024)S(1)} collective-permute-done((f32[2048]{0:T(1024)S(1)}, f32[2048]{0:T(1024)S(1)}, u32[]{:S(2)}, u32[]{:S(2)}) %collective-permute-start.1) | collective-permute-done | bytes 8224 | tf_op jit(solution)/shard_map/while/body/eval_jaxpr/ppermute | solution.py:69
  485.6 18.7 %collective-permute-done.1 = f32[2048]{0:T(1024)S(1)} collective-permute-done((f32[2048]{0:T(1024)S(1)}, f32[2048]{0:T(1024)S(1)}, u32[]{:S(2)}, u32[]{:S(2)}) %collective-permute-start.1) | collective-permute-done | bytes 8224 | tf_op jit(solution)/shard_map/while/body/eval_jaxpr/ppermute | solution.py:69
  519.9 19.5 %collective-permute-done.1 = f32[2048]{0:T(1024)S(1)} collective-permute-done((f32[2048]{0:T(1024)S(1)}, f32[2048]{0:T(1024)S(1)}, u32[]{:S(2)}, u32[]{:S(2)}) %collective-permute-start.1) | collective-permute-done | bytes 8224 | tf_op jit(solution)/shard_map/while/body/eval_jaxpr/ppermute | solution.py:69
  554.1 19.5 %collective-permute-done.1 = f32[2048]{0:T(1024)S(1)} collective-permute-done((f32[2048]{0:T(1024)S(1)}, f32[2048]{0:T(1024)S(1)}, u32[]{:S(2)}, u32[]{:S(2)}) %collective-permute-start.1) | collective-permute-done | bytes 8224 | tf_op jit(solution)/shard_map/while/body/eval_jaxpr/ppermute | solution.py:69
  588.5 19.5 %collective-permute-done.1 = f32[2048]{0:T(1024)S(1)} collective-permute-done((f32[2048]{0:T(1024)S(1)}, f32[2048]{0:T(1024)S(1)}, u32[]{:S(2)}, u32[]{:S(2)}) %collective-permute-start.1) | collective-permute-done | bytes 8224 | tf_op jit(solution)/shard_map/while/body/eval_jaxpr/ppermute | solution.py:69
  623.5 19.5 %collective-permute-done.1 = f32[2048]{0:T(1024)S(1)} collective-permute-done((f32[2048]{0:T(1024)S(1)}, f32[2048]{0:T(1024)S(1)}, u32[]{:S(2)}, u32[]{:S(2)}) %collective-permute-start.1) | collective-permute-done | bytes 8224 | tf_op jit(solution)/shard_map/while/body/eval_jaxpr/ppermute | solution.py:69
  659.0 19.5 %collective-permute-done.1 = f32[2048]{0:T(1024)S(1)} collective-permute-done((f32[2048]{0:T(1024)S(1)}, f32[2048]{0:T(1024)S(1)}, u32[]{:S(2)}, u32[]{:S(2)}) %collective-permute-start.1) | collective-permute-done | bytes 8224 | tf_op jit(solution)/shard_map/while/body/eval_jaxpr/ppermute | solution.py:69
  695.1 19.5 %collective-permute-done.1 = f32[2048]{0:T(1024)S(1)} collective-permute-done((f32[2048]{0:T(1024)S(1)}, f32[2048]{0:T(1024)S(1)}, u32[]{:S(2)}, u32[]{:S(2)}) %collective-permute-start.1) | collective-permute-done | bytes 8224 | tf_op jit(solution)/shard_map/while/body/eval_jaxpr/ppermute | solution.py:69
  731.8 19.5 %collective-permute-done.1 = f32[2048]{0:T(1024)S(1)} collective-permute-done((f32[2048]{0:T(1024)S(1)}, f32[2048]{0:T(1024)S(1)}, u32[]{:S(2)}, u32[]{:S(2)}) %collective-permute-start.1) | collective-permute-done | bytes 8224 | tf_op jit(solution)/shard_map/while/body/eval_jaxpr/ppermute | solution.py:69
  769.2 19.5 %collective-permute-done.1 = f32[2048]{0:T(1024)S(1)} collective-permute-done((f32[2048]{0:T(1024)S(1)}, f32[2048]{0:T(1024)S(1)}, u32[]{:S(2)}, u32[]{:S(2)}) %collective-permute-start.1) | collective-permute-done | bytes 8224 | tf_op jit(solution)/shard_map/while/body/eval_jaxpr/ppermute | solution.py:69
  807.2 19.5 %collective-permute-done.1 = f32[2048]{0:T(1024)S(1)} collective-permute-done((f32[2048]{0:T(1024)S(1)}, f32[2048]{0:T(1024)S(1)}, u32[]{:S(2)}, u32[]{:S(2)}) %collective-permute-start.1) | collective-permute-done | bytes 8224 | tf_op jit(solution)/shard_map/while/body/eval_jaxpr/ppermute | solution.py:69
  845.9 19.5 %collective-permute-done.1 = f32[2048]{0:T(1024)S(1)} collective-permute-done((f32[2048]{0:T(1024)S(1)}, f32[2048]{0:T(1024)S(1)}, u32[]{:S(2)}, u32[]{:S(2)}) %collective-permute-start.1) | collective-permute-done | bytes 8224 | tf_op jit(solution)/shard_map/while/body/eval_jaxpr/ppermute | solution.py:69
  885.2 19.5 %collective-permute-done.1 = f32[2048]{0:T(1024)S(1)} collective-permute-done((f32[2048]{0:T(1024)S(1)}, f32[2048]{0:T(1024)S(1)}, u32[]{:S(2)}, u32[]{:S(2)}) %collective-permute-start.1) | collective-permute-done | bytes 8224 | tf_op jit(solution)/shard_map/while/body/eval_jaxpr/ppermute | solution.py:69
  925.3 19.5 %collective-permute-done.1 = f32[2048]{0:T(1024)S(1)} collective-permute-done((f32[2048]{0:T(1024)S(1)}, f32[2048]{0:T(1024)S(1)}, u32[]{:S(2)}, u32[]{:S(2)}) %collective-permute-start.1) | collective-permute-done | bytes 8224 | tf_op jit(solution)/shard_map/while/body/eval_jaxpr/ppermute | solution.py:69
  966.1 19.5 %collective-permute-done.1 = f32[2048]{0:T(1024)S(1)} collective-permute-done((f32[2048]{0:T(1024)S(1)}, f32[2048]{0:T(1024)S(1)}, u32[]{:S(2)}, u32[]{:S(2)}) %collective-permute-start.1) | collective-permute-done | bytes 8224 | tf_op jit(solution)/shard_map/while/body/eval_jaxpr/ppermute | solution.py:69
  1007.6 19.5 %collective-permute-done.1 = f32[2048]{0:T(1024)S(1)} collective-permute-done((f32[2048]{0:T(1024)S(1)}, f32[2048]{0:T(1024)S(1)}, u32[]{:S(2)}, u32[]{:S(2)}) %collective-permute-start.1) | collective-permute-done | bytes 8224 | tf_op jit(solution)/shard_map/while/body/eval_jaxpr/ppermute | solution.py:69
  1049.7 19.5 %collective-permute-done.1 = f32[2048]{0:T(1024)S(1)} collective-permute-done((f32[2048]{0:T(1024)S(1)}, f32[2048]{0:T(1024)S(1)}, u32[]{:S(2)}, u32[]{:S(2)}) %collective-permute-start.1) | collective-permute-done | bytes 8224 | tf_op jit(solution)/shard_map/while/body/eval_jaxpr/ppermute | solution.py:69
  1092.6 19.5 %collective-permute-done.1 = f32[2048]{0:T(1024)S(1)} collective-permute-done((f32[2048]{0:T(1024)S(1)}, f32[2048]{0:T(1024)S(1)}, u32[]{:S(2)}, u32[]{:S(2)}) %collective-permute-start.1) | collective-permute-done | bytes 8224 | tf_op jit(solution)/shard_map/while/body/eval_jaxpr/ppermute | solution.py:69
  1136.2 19.5 %collective-permute-done.1 = f32[2048]{0:T(1024)S(1)} collective-permute-done((f32[2048]{0:T(1024)S(1)}, f32[2048]{0:T(1024)S(1)}, u32[]{:S(2)}, u32[]{:S(2)}) %collective-permute-start.1) | collective-permute-done | bytes 8224 | tf_op jit(solution)/shard_map/while/body/eval_jaxpr/ppermute | solution.py:69
  1180.5 18.7 %collective-permute-done.6 = bf16[2048,128]{1,0:T(8,128)(2,1)S(1)} collective-permute-done((bf16[2048,128]{1,0:T(8,128)(2,1)S(1)}, bf16[2048,128]{1,0:T(8,128)(2,1)S(1)}, u32[]{:S(2)}, u32[]{:S(2)}) %collective-permute-start.6) | collective-permute-done | bytes 524320 | tf_op jit(solution)/shard_map/ppermute | solution.py:77
  1223.3 34.0 %reduce-scatter.2.cloned.1.call-done = f32[1024,128]{1,0:T(8,128)} async-done(((f32[2048,128]{1,0:T(8,128)}), f32[1024,128]{1,0:T(8,128)}) %reduce-scatter.2.cloned.1.call-update) | async-done | bytes 524304 | tf_op jit(solution)/shard_map/reduce_scatter | solution.py:82
  1261.0 70.1 %psum.7 = f32[1]{0:T(128)} all-reduce(f32[1]{0:T(128)} %bitcast.1), channel_id=1, replica_groups=mesh['sys'=1,'col'=2,'seg'=64] {'seg','col'}, use_global_device_ids=true, to_apply=%region_19.20 | all-reduce | flops 1 | bytes 8 | tf_op jit(solution)/shard_map/psum | solution.py:84
  (432 shorter events, 677.1 us)
Async XLA Ops:
  7.2 1250.2 %reduce-scatter.2.cloned.1.call-start = ((), (), s32[]{:S(2)}) async-start(), calls=%async_computation.1 | async-start | bytes 1572864 | tf_op jit(solution)/shard_map/reduce_scatter | solution.py:82
  44.5 40.0 %collective-permute-start.2 = (f32[2048,128]{1,0:T(8,128)}, f32[2048,128]{1,0:T(8,128)S(1)}, u32[]{:S(2)}, u32[]{:S(2)}) collective-permute-start(f32[2048,128]{1,0:T(8,128)} %get-tuple-element.182), channel_id=1, source_target_pairs={{0,1},{1,2},{2,3},{3,4},{4,5},{5,6},{6,7},{7,8},{8,9},{9,10},{10,1... | collective-permute-start | bytes 3145736 | tf_op jit(solution)/shard_map/while/body/eval_jaxpr/ppermute | solution.py:70
  86.9 38.7 %collective-permute-start.2 = (f32[2048,128]{1,0:T(8,128)}, f32[2048,128]{1,0:T(8,128)S(1)}, u32[]{:S(2)}, u32[]{:S(2)}) collective-permute-start(f32[2048,128]{1,0:T(8,128)} %get-tuple-element.182), channel_id=1, source_target_pairs={{0,1},{1,2},{2,3},{3,4},{4,5},{5,6},{6,7},{7,8},{8,9},{9,10},{10,1... | collective-permute-start | bytes 3145736 | tf_op jit(solution)/shard_map/while/body/eval_jaxpr/ppermute | solution.py:70
  128.1 37.4 %collective-permute-start.2 = (f32[2048,128]{1,0:T(8,128)}, f32[2048,128]{1,0:T(8,128)S(1)}, u32[]{:S(2)}, u32[]{:S(2)}) collective-permute-start(f32[2048,128]{1,0:T(8,128)} %get-tuple-element.182), channel_id=1, source_target_pairs={{0,1},{1,2},{2,3},{3,4},{4,5},{5,6},{6,7},{7,8},{8,9},{9,10},{10,1... | collective-permute-start | bytes 3145736 | tf_op jit(solution)/shard_map/while/body/eval_jaxpr/ppermute | solution.py:70
  168.0 36.1 %collective-permute-start.2 = (f32[2048,128]{1,0:T(8,128)}, f32[2048,128]{1,0:T(8,128)S(1)}, u32[]{:S(2)}, u32[]{:S(2)}) collective-permute-start(f32[2048,128]{1,0:T(8,128)} %get-tuple-element.182), channel_id=1, source_target_pairs={{0,1},{1,2},{2,3},{3,4},{4,5},{5,6},{6,7},{7,8},{8,9},{9,10},{10,1... | collective-permute-start | bytes 3145736 | tf_op jit(solution)/shard_map/while/body/eval_jaxpr/ppermute | solution.py:70
  206.6 34.8 %collective-permute-start.2 = (f32[2048,128]{1,0:T(8,128)}, f32[2048,128]{1,0:T(8,128)S(1)}, u32[]{:S(2)}, u32[]{:S(2)}) collective-permute-start(f32[2048,128]{1,0:T(8,128)} %get-tuple-element.182), channel_id=1, source_target_pairs={{0,1},{1,2},{2,3},{3,4},{4,5},{5,6},{6,7},{7,8},{8,9},{9,10},{10,1... | collective-permute-start | bytes 3145736 | tf_op jit(solution)/shard_map/while/body/eval_jaxpr/ppermute | solution.py:70
  243.9 33.5 %collective-permute-start.2 = (f32[2048,128]{1,0:T(8,128)}, f32[2048,128]{1,0:T(8,128)S(1)}, u32[]{:S(2)}, u32[]{:S(2)}) collective-permute-start(f32[2048,128]{1,0:T(8,128)} %get-tuple-element.182), channel_id=1, source_target_pairs={{0,1},{1,2},{2,3},{3,4},{4,5},{5,6},{6,7},{7,8},{8,9},{9,10},{10,1... | collective-permute-start | bytes 3145736 | tf_op jit(solution)/shard_map/while/body/eval_jaxpr/ppermute | solution.py:70
  279.8 32.1 %collective-permute-start.2 = (f32[2048,128]{1,0:T(8,128)}, f32[2048,128]{1,0:T(8,128)S(1)}, u32[]{:S(2)}, u32[]{:S(2)}) collective-permute-start(f32[2048,128]{1,0:T(8,128)} %get-tuple-element.182), channel_id=1, source_target_pairs={{0,1},{1,2},{2,3},{3,4},{4,5},{5,6},{6,7},{7,8},{8,9},{9,10},{10,1... | collective-permute-start | bytes 3145736 | tf_op jit(solution)/shard_map/while/body/eval_jaxpr/ppermute | solution.py:70
  347.6 32.1 %collective-permute-start.2 = (f32[2048,128]{1,0:T(8,128)}, f32[2048,128]{1,0:T(8,128)S(1)}, u32[]{:S(2)}, u32[]{:S(2)}) collective-permute-start(f32[2048,128]{1,0:T(8,128)} %get-tuple-element.182), channel_id=1, source_target_pairs={{0,1},{1,2},{2,3},{3,4},{4,5},{5,6},{6,7},{7,8},{8,9},{9,10},{10,1... | collective-permute-start | bytes 3145736 | tf_op jit(solution)/shard_map/while/body/eval_jaxpr/ppermute | solution.py:70
  382.2 32.1 %collective-permute-start.2 = (f32[2048,128]{1,0:T(8,128)}, f32[2048,128]{1,0:T(8,128)S(1)}, u32[]{:S(2)}, u32[]{:S(2)}) collective-permute-start(f32[2048,128]{1,0:T(8,128)} %get-tuple-element.182), channel_id=1, source_target_pairs={{0,1},{1,2},{2,3},{3,4},{4,5},{5,6},{6,7},{7,8},{8,9},{9,10},{10,1... | collective-permute-start | bytes 3145736 | tf_op jit(solution)/shard_map/while/body/eval_jaxpr/ppermute | solution.py:70
  416.7 32.0 %collective-permute-start.2 = (f32[2048,128]{1,0:T(8,128)}, f32[2048,128]{1,0:T(8,128)S(1)}, u32[]{:S(2)}, u32[]{:S(2)}) collective-permute-start(f32[2048,128]{1,0:T(8,128)} %get-tuple-element.182), channel_id=1, source_target_pairs={{0,1},{1,2},{2,3},{3,4},{4,5},{5,6},{6,7},{7,8},{8,9},{9,10},{10,1... | collective-permute-start | bytes 3145736 | tf_op jit(solution)/shard_map/while/body/eval_jaxpr/ppermute | solution.py:70
  451.2 31.9 %collective-permute-start.2 = (f32[2048,128]{1,0:T(8,128)}, f32[2048,128]{1,0:T(8,128)S(1)}, u32[]{:S(2)}, u32[]{:S(2)}) collective-permute-start(f32[2048,128]{1,0:T(8,128)} %get-tuple-element.182), channel_id=1, source_target_pairs={{0,1},{1,2},{2,3},{3,4},{4,5},{5,6},{6,7},{7,8},{8,9},{9,10},{10,1... | collective-permute-start | bytes 3145736 | tf_op jit(solution)/shard_map/while/body/eval_jaxpr/ppermute | solution.py:70
  485.6 31.9 %collective-permute-start.2 = (f32[2048,128]{1,0:T(8,128)}, f32[2048,128]{1,0:T(8,128)S(1)}, u32[]{:S(2)}, u32[]{:S(2)}) collective-permute-start(f32[2048,128]{1,0:T(8,128)} %get-tuple-element.182), channel_id=1, source_target_pairs={{0,1},{1,2},{2,3},{3,4},{4,5},{5,6},{6,7},{7,8},{8,9},{9,10},{10,1... | collective-permute-start | bytes 3145736 | tf_op jit(solution)/shard_map/while/body/eval_jaxpr/ppermute | solution.py:70
  519.9 31.8 %collective-permute-start.2 = (f32[2048,128]{1,0:T(8,128)}, f32[2048,128]{1,0:T(8,128)S(1)}, u32[]{:S(2)}, u32[]{:S(2)}) collective-permute-start(f32[2048,128]{1,0:T(8,128)} %get-tuple-element.182), channel_id=1, source_target_pairs={{0,1},{1,2},{2,3},{3,4},{4,5},{5,6},{6,7},{7,8},{8,9},{9,10},{10,1... | collective-permute-start | bytes 3145736 | tf_op jit(solution)/shard_map/while/body/eval_jaxpr/ppermute | solution.py:70
  554.1 31.9 %collective-permute-start.2 = (f32[2048,128]{1,0:T(8,128)}, f32[2048,128]{1,0:T(8,128)S(1)}, u32[]{:S(2)}, u32[]{:S(2)}) collective-permute-start(f32[2048,128]{1,0:T(8,128)} %get-tuple-element.182), channel_id=1, source_target_pairs={{0,1},{1,2},{2,3},{3,4},{4,5},{5,6},{6,7},{7,8},{8,9},{9,10},{10,1... | collective-permute-start | bytes 3145736 | tf_op jit(solution)/shard_map/while/body/eval_jaxpr/ppermute | solution.py:70
  588.5 32.5 %collective-permute-start.2 = (f32[2048,128]{1,0:T(8,128)}, f32[2048,128]{1,0:T(8,128)S(1)}, u32[]{:S(2)}, u32[]{:S(2)}) collective-permute-start(f32[2048,128]{1,0:T(8,128)} %get-tuple-element.182), channel_id=1, source_target_pairs={{0,1},{1,2},{2,3},{3,4},{4,5},{5,6},{6,7},{7,8},{8,9},{9,10},{10,1... | collective-permute-start | bytes 3145736 | tf_op jit(solution)/shard_map/while/body/eval_jaxpr/ppermute | solution.py:70
  623.4 33.1 %collective-permute-start.2 = (f32[2048,128]{1,0:T(8,128)}, f32[2048,128]{1,0:T(8,128)S(1)}, u32[]{:S(2)}, u32[]{:S(2)}) collective-permute-start(f32[2048,128]{1,0:T(8,128)} %get-tuple-element.182), channel_id=1, source_target_pairs={{0,1},{1,2},{2,3},{3,4},{4,5},{5,6},{6,7},{7,8},{8,9},{9,10},{10,1... | collective-permute-start | bytes 3145736 | tf_op jit(solution)/shard_map/while/body/eval_jaxpr/ppermute | solution.py:70
  659.0 33.7 %collective-permute-start.2 = (f32[2048,128]{1,0:T(8,128)}, f32[2048,128]{1,0:T(8,128)S(1)}, u32[]{:S(2)}, u32[]{:S(2)}) collective-permute-start(f32[2048,128]{1,0:T(8,128)} %get-tuple-element.182), channel_id=1, source_target_pairs={{0,1},{1,2},{2,3},{3,4},{4,5},{5,6},{6,7},{7,8},{8,9},{9,10},{10,1... | collective-permute-start | bytes 3145736 | tf_op jit(solution)/shard_map/while/body/eval_jaxpr/ppermute | solution.py:70
  695.1 34.3 %collective-permute-start.2 = (f32[2048,128]{1,0:T(8,128)}, f32[2048,128]{1,0:T(8,128)S(1)}, u32[]{:S(2)}, u32[]{:S(2)}) collective-permute-start(f32[2048,128]{1,0:T(8,128)} %get-tuple-element.182), channel_id=1, source_target_pairs={{0,1},{1,2},{2,3},{3,4},{4,5},{5,6},{6,7},{7,8},{8,9},{9,10},{10,1... | collective-permute-start | bytes 3145736 | tf_op jit(solution)/shard_map/while/body/eval_jaxpr/ppermute | solution.py:70
  731.8 34.9 %collective-permute-start.2 = (f32[2048,128]{1,0:T(8,128)}, f32[2048,128]{1,0:T(8,128)S(1)}, u32[]{:S(2)}, u32[]{:S(2)}) collective-permute-start(f32[2048,128]{1,0:T(8,128)} %get-tuple-element.182), channel_id=1, source_target_pairs={{0,1},{1,2},{2,3},{3,4},{4,5},{5,6},{6,7},{7,8},{8,9},{9,10},{10,1... | collective-permute-start | bytes 3145736 | tf_op jit(solution)/shard_map/while/body/eval_jaxpr/ppermute | solution.py:70
  769.2 35.6 %collective-permute-start.2 = (f32[2048,128]{1,0:T(8,128)}, f32[2048,128]{1,0:T(8,128)S(1)}, u32[]{:S(2)}, u32[]{:S(2)}) collective-permute-start(f32[2048,128]{1,0:T(8,128)} %get-tuple-element.182), channel_id=1, source_target_pairs={{0,1},{1,2},{2,3},{3,4},{4,5},{5,6},{6,7},{7,8},{8,9},{9,10},{10,1... | collective-permute-start | bytes 3145736 | tf_op jit(solution)/shard_map/while/body/eval_jaxpr/ppermute | solution.py:70
  807.2 36.2 %collective-permute-start.2 = (f32[2048,128]{1,0:T(8,128)}, f32[2048,128]{1,0:T(8,128)S(1)}, u32[]{:S(2)}, u32[]{:S(2)}) collective-permute-start(f32[2048,128]{1,0:T(8,128)} %get-tuple-element.182), channel_id=1, source_target_pairs={{0,1},{1,2},{2,3},{3,4},{4,5},{5,6},{6,7},{7,8},{8,9},{9,10},{10,1... | collective-permute-start | bytes 3145736 | tf_op jit(solution)/shard_map/while/body/eval_jaxpr/ppermute | solution.py:70
  845.9 36.9 %collective-permute-start.2 = (f32[2048,128]{1,0:T(8,128)}, f32[2048,128]{1,0:T(8,128)S(1)}, u32[]{:S(2)}, u32[]{:S(2)}) collective-permute-start(f32[2048,128]{1,0:T(8,128)} %get-tuple-element.182), channel_id=1, source_target_pairs={{0,1},{1,2},{2,3},{3,4},{4,5},{5,6},{6,7},{7,8},{8,9},{9,10},{10,1... | collective-permute-start | bytes 3145736 | tf_op jit(solution)/shard_map/while/body/eval_jaxpr/ppermute | solution.py:70
  885.2 37.6 %collective-permute-start.2 = (f32[2048,128]{1,0:T(8,128)}, f32[2048,128]{1,0:T(8,128)S(1)}, u32[]{:S(2)}, u32[]{:S(2)}) collective-permute-start(f32[2048,128]{1,0:T(8,128)} %get-tuple-element.182), channel_id=1, source_target_pairs={{0,1},{1,2},{2,3},{3,4},{4,5},{5,6},{6,7},{7,8},{8,9},{9,10},{10,1... | collective-permute-start | bytes 3145736 | tf_op jit(solution)/shard_map/while/body/eval_jaxpr/ppermute | solution.py:70
  925.3 38.3 %collective-permute-start.2 = (f32[2048,128]{1,0:T(8,128)}, f32[2048,128]{1,0:T(8,128)S(1)}, u32[]{:S(2)}, u32[]{:S(2)}) collective-permute-start(f32[2048,128]{1,0:T(8,128)} %get-tuple-element.182), channel_id=1, source_target_pairs={{0,1},{1,2},{2,3},{3,4},{4,5},{5,6},{6,7},{7,8},{8,9},{9,10},{10,1... | collective-permute-start | bytes 3145736 | tf_op jit(solution)/shard_map/while/body/eval_jaxpr/ppermute | solution.py:70
  966.1 39.0 %collective-permute-start.2 = (f32[2048,128]{1,0:T(8,128)}, f32[2048,128]{1,0:T(8,128)S(1)}, u32[]{:S(2)}, u32[]{:S(2)}) collective-permute-start(f32[2048,128]{1,0:T(8,128)} %get-tuple-element.182), channel_id=1, source_target_pairs={{0,1},{1,2},{2,3},{3,4},{4,5},{5,6},{6,7},{7,8},{8,9},{9,10},{10,1... | collective-permute-start | bytes 3145736 | tf_op jit(solution)/shard_map/while/body/eval_jaxpr/ppermute | solution.py:70
  1007.6 39.7 %collective-permute-start.2 = (f32[2048,128]{1,0:T(8,128)}, f32[2048,128]{1,0:T(8,128)S(1)}, u32[]{:S(2)}, u32[]{:S(2)}) collective-permute-start(f32[2048,128]{1,0:T(8,128)} %get-tuple-element.182), channel_id=1, source_target_pairs={{0,1},{1,2},{2,3},{3,4},{4,5},{5,6},{6,7},{7,8},{8,9},{9,10},{10,1... | collective-permute-start | bytes 3145736 | tf_op jit(solution)/shard_map/while/body/eval_jaxpr/ppermute | solution.py:70
  1049.7 40.4 %collective-permute-start.2 = (f32[2048,128]{1,0:T(8,128)}, f32[2048,128]{1,0:T(8,128)S(1)}, u32[]{:S(2)}, u32[]{:S(2)}) collective-permute-start(f32[2048,128]{1,0:T(8,128)} %get-tuple-element.182), channel_id=1, source_target_pairs={{0,1},{1,2},{2,3},{3,4},{4,5},{5,6},{6,7},{7,8},{8,9},{9,10},{10,1... | collective-permute-start | bytes 3145736 | tf_op jit(solution)/shard_map/while/body/eval_jaxpr/ppermute | solution.py:70
  1092.6 41.1 %collective-permute-start.2 = (f32[2048,128]{1,0:T(8,128)}, f32[2048,128]{1,0:T(8,128)S(1)}, u32[]{:S(2)}, u32[]{:S(2)}) collective-permute-start(f32[2048,128]{1,0:T(8,128)} %get-tuple-element.182), channel_id=1, source_target_pairs={{0,1},{1,2},{2,3},{3,4},{4,5},{5,6},{6,7},{7,8},{8,9},{9,10},{10,1... | collective-permute-start | bytes 3145736 | tf_op jit(solution)/shard_map/while/body/eval_jaxpr/ppermute | solution.py:70
  1136.2 41.7 %collective-permute-start.2 = (f32[2048,128]{1,0:T(8,128)}, f32[2048,128]{1,0:T(8,128)S(1)}, u32[]{:S(2)}, u32[]{:S(2)}) collective-permute-start(f32[2048,128]{1,0:T(8,128)} %get-tuple-element.182), channel_id=1, source_target_pairs={{0,1},{1,2},{2,3},{3,4},{4,5},{5,6},{6,7},{7,8},{8,9},{9,10},{10,1... | collective-permute-start | bytes 3145736 | tf_op jit(solution)/shard_map/while/body/eval_jaxpr/ppermute | solution.py:70
  1180.5 41.5 %collective-permute-start.7 = (f32[2048,128]{1,0:T(8,128)}, f32[2048,128]{1,0:T(8,128)S(1)}, u32[]{:S(2)}, u32[]{:S(2)}) collective-permute-start(f32[2048,128]{1,0:T(8,128)} %get-tuple-element.56), channel_id=1, source_target_pairs={{0,1},{1,2},{2,3},{3,4},{4,5},{5,6},{6,7},{7,8},{8,9},{9,10},{10,1... | collective-permute-start | bytes 3145736 | tf_op jit(solution)/shard_map/ppermute | solution.py:79
  1257.3 77.1 %collective-permute-start.8 = (f32[1024,128]{1,0:T(8,128)}, f32[1024,128]{1,0:T(8,128)S(1)}, u32[]{:S(2)}, u32[]{:S(2)}) collective-permute-start(f32[1024,128]{1,0:T(8,128)} %reduce-scatter.2.cloned.1.call-done), channel_id=1, source_target_pairs={{0,32},{1,33},{2,34},{3,35},{4,36},{5,37},{6,38},{7,39},{8,40},{9,... | collective-permute-start | bytes 1572872 | tf_op jit(solution)/shard_map/ppermute | solution.py:83
  (99 other events, 1508.9 us)
Sparse Core Ops, SparseCore 0:
  1223.5 33.8 reduce-scatter.1
where the time goes:
time: 1340 us
  waiting for transfers between devices  802 us (60%)
  matrix products  403 us (30%)
  blocking collectives  75.3 us (6%)
  loops' own time  20.7 us (2%)
  between operations  16.1 us (1%)
  other arithmetic  14.9 us (1%)
    ppermute x30, waiting for transfers between devices, step_body(): q_vis = lax.ppermute(q_vis, 'seg', forward)  533 us
    dot_general x33, matrix products, pair_weights(): lax.dot_general(x_host, x_vis, (((1,), (1,)), ((), ())), preferred_elemen...  207 us
    ppermute x30, waiting for transfers between devices, step_body(): reaction = lax.ppermute(reaction, 'seg', forward)  201 us
    dot_general x33, matrix products, host_terms(): pulled = jnp.dot(w_low, x_vis, preferred_element_type=jnp.float32)  116 us
    dot_general x32, matrix products, visitor_terms(): lax.dot_general(w_low, x_host, (((0,), (0,)), ((), ())), preferred_elemen...  79.5 us
    psum x1, blocking collectives, per_device(): energy = lax.psum(energy, ('seg', 'col'))  70.1 us
    reduce_scatter x1, waiting for transfers between devices, per_device(): lax.psum_scatter(reaction, 'col', scatter_dimension=0, tiled=True)  34 us
  transfers between devices with their start and end apart: 97, of which 64 were waited for; matrix products, arithmetic and copies ran while one was open for 25% of the time, Pallas kernels for 0%

commit v1 on v0

v1 whole, which is shorter than its diff:
```python
import functools
import math

import jax
import jax.numpy as jnp
from jax import lax
from jax.experimental import pallas as pl
from jax.experimental.pallas import tpu as pltpu
from jax.sharding import PartitionSpec as P

F32 = jnp.float32
BF16 = jnp.bfloat16
ROW_AXES = ('sys', 'seg', 'col')
GA, GT = 16, 8
OWN = 1024
TB = 256
NB = OWN // TB
EXT = 48
PR = 64
NP = TB // PR
HALF_SHELL = GA // 2


def grid_of(seg, col):
    z, y, x = seg // 16, (seg // 4) % 4, seg % 4
    ya = y // 2
    yb = (ya + y % 2) % 2
    return (z * 2 + ya) * 2 + col, x * 2 + yb


def shift_pairs(da, dt):
    at = {grid_of(seg, col): col * 64 + seg for seg in range(64) for col in range(2)}
    return [(at[((a + da) % GA, (t + dt) % GT)], at[(a, t)]) for a in range(GA) for t in range(GT)]


def split3(v):
    hi = lax.reduce_precision(v, 8, 7)
    mid = lax.reduce_precision(v - hi, 8, 7)
    lo = lax.reduce_precision(v - hi - mid, 8, 7)
    return [p.astype(BF16) for p in (hi, mid, lo)]


def pair_kernel(scale, flags, xe, fu, fv, en, xi, xv, xtv, qu, qv, su, sv, *wsc):
    def ext_row(b, m, ib):
        row = xe[b, OWN + 8 * m:OWN + 8 * (m + 1), :].astype(F32)
        sel = lax.broadcasted_iota(jnp.int32, (8, 128), 0)
        lo = jnp.sum(jnp.where(sel == 2 * ib, row, 0.0), axis=0, keepdims=True)
        hi = jnp.sum(jnp.where(sel == 2 * ib + 1, row, 0.0), axis=0, keepdims=True)
        return jnp.concatenate([lo, hi], axis=1)

    def aug_rows(b, ib, s_first):
        r = lax.broadcasted_iota(jnp.int32, (128, TB), 0)
        out = jnp.where((r >= 3 - s_first) & (r < 6 - s_first), 1.0, 0.0)
        for m in range(3):
            out = jnp.where(r == s_first + m, ext_row(b, m, ib), out)
        return out.astype(BF16)

    def charge_row(b, ib):
        return (ext_row(b, 3, ib) + ext_row(b, 4, ib)) + ext_row(b, 5, ib)

    def prep_u(n, _):
        u, ib = n // NB, n % NB
        xt = xe[u, pl.ds(pl.multiple_of(ib * TB, TB), TB), :].T
        xi[n, 0:128, :] = xt
        xi[n, 128:256, :] = aug_rows(u, ib, 3)
        qu[n] = jnp.broadcast_to(charge_row(u, ib), (8, TB))
        return 0

    def prep_v(n, _):
        v, ib = n // NB, n % NB
        b = jnp.where(v == 0, 0, v + GT - 1)
        xb = xe[b, pl.ds(pl.multiple_of(ib * TB, TB), TB), :]
        xv[n, :, 0:128] = xb
        xv[n, :, 128:256] = aug_rows(b, ib, 0).T
        xtv[n] = xb.T
        qv[n] = jnp.broadcast_to(charge_row(b, ib), (128, TB)).T
        sv[n] = jnp.zeros((TB, 128), F32)
        fv[n] = jnp.zeros((128, TB), F32)
        return 0

    lax.fori_loop(0, GT * NB, prep_u, 0)
    lax.fori_loop(0, (HALF_SHELL + 1) * NB, prep_v, 0)

    def run(*accs):
        G = lambda q, k, p: accs[(q * 2 + k) * NP + p]
        F = lambda q, k: accs[4 * NP + q * 2 + k]
        FJ = lambda q, s: accs[4 * NP + 4 + q * 2 + s]

        def issue_g(u, bj, k):
            for q in range(2):
                pltpu.matmul_push_rhs(xi[NB * u + 2 * k + q], staging_register=1, mxu_index=q)
            for p in range(NP):
                lhs = xv[bj, p * PR:(p + 1) * PR, :]
                for q in range(2):
                    pltpu.matmul_acc_lhs(G(q, k, p), lhs, load_staged_rhs=1 if p == 0 else None)

        def elem(u, bj, k, masked):
            cs = [None, None]
            for p in range(NP):
                qvr = qv[bj, p * PR:(p + 1) * PR, :]
                rs = None
                for q in range(2):
                    ib = NB * u + 2 * k + q
                    quv = qu[ib, 0:1, :]
                    g = pltpu.matmul_pop(G(q, k, p))
                    e = jnp.exp2(jnp.minimum(g * scale, 0.0))
                    w0 = (qvr * quv[:, :128]) * e[:, :128]
                    w1 = (qvr * quv[:, 128:]) * e[:, 128:]
                    w = jnp.concatenate([w0, w1], axis=1)
                    if masked:
                        jj = bj * TB + p * PR + lax.broadcasted_iota(jnp.int32, (PR, TB), 0)
                        ii = ib * TB + lax.broadcasted_iota(jnp.int32, (PR, TB), 1)
                        w = jnp.where(jj < ii, w, 0.0)
                        w0, w1 = w[:, :128], w[:, 128:]
                    wsc[q * 2 + k][p * PR:(p + 1) * PR, :] = w.astype(BF16)
                    c = jnp.sum(w.reshape(PR // 8, 8, TB), axis=0)
                    cs[q] = c if cs[q] is None else cs[q] + c
                    rs = w0 + w1 if rs is None else rs + (w0 + w1)
                sv[bj, p * PR:(p + 1) * PR, :] += rs
            for q in range(2):
                su[NB * u + 2 * k + q] += cs[q]

        def force(u, bj, k, s):
            for q in range(2):
                pltpu.matmul_push_rhs(wsc[q * 2 + k][...], staging_register=1, mxu_index=q)
            lhs = xtv[bj]
            for q in range(2):
                pltpu.matmul_acc_lhs(F(q, k), lhs, load_staged_rhs=1)
            for q in range(2):
                pltpu.matmul_push_rhs(wsc[q * 2 + k][...], staging_register=0, mxu_index=q, transpose=True)
            for q in range(2):
                pltpu.matmul_acc_lhs(FJ(q, s), xi[NB * u + 2 * k + q, 0:128, :], load_staged_rhs=0)

        def flush(bj, s):
            fv[bj] += pltpu.matmul_pop(FJ(0, s)) + pltpu.matmul_pop(FJ(1, s))

        def sweep(u, start, count, masked):
            last = start + count - 1
            for k in range(2):
                issue_g(u, start, k)
            for q in range(2):
                wsc[q * 2 + 1][...] = jnp.zeros((TB, TB), BF16)

            def steps(base, unroll):
                for n in range(unroll):
                    bj, s = base + n, n % 2
                    nxt = jnp.minimum(bj + 1, last)
                    prv = jnp.maximum(bj - 1, start)
                    for k in range(2):
                        elem(u, bj, k, masked)
                        force(u, bj if k else prv, 1 - k, s if k else 1 - s)
                        issue_g(u, nxt, k)
                    flush(prv, 1 - s)

            n8 = 0
            if not masked:
                n8 = count // 8

                def body8(h, _):
                    steps(start + 8 * h, 8)
                    return 0
                lax.fori_loop(0, n8, body8, 0)

            def body4(h, _):
                steps(start + 8 * n8 + 4 * h, 4)
                return 0
            lax.fori_loop(0, count // 4 - 2 * n8, body4, 0)
            force(u, last, 1, 1)
            flush(last, 1)
            for k in range(2):
                for q in range(2):
                    for p in range(NP):
                        pltpu.matmul_pop(G(q, k, p))

        def finish(u):
            for k in range(2):
                for q in range(2):
                    n = NB * u + 2 * k + q
                    tot = jnp.sum(su[n], axis=0, keepdims=True)
                    fu[n] = tot * xi[n, 0:128, :].astype(F32) - pltpu.matmul_pop(F(q, k))

        for n in range(GT * NB):
            su[n] = jnp.zeros((8, TB), F32)
        sweep(0, 0, NB, True)
        def host(u, _):
            start = jnp.where((u == 0) | (u > 4), 1, jnp.where(u == 4, flags[1], 0))
            stop = jnp.where(u == 0, HALF_SHELL + flags[0], jnp.where(u > 4, HALF_SHELL, jnp.where(u == 4, HALF_SHELL + flags[1], HALF_SHELL + 1)))
            sweep(u, NB * start, NB * (stop - start), False)
            finish(u)
            return 0
        lax.fori_loop(0, GT, host, 0)

    specs = [pltpu.ACC(q)((PR, TB), F32) for q in range(2) for k in range(2) for p in range(NP)]
    specs += [pltpu.ACC(q)((128, TB), F32) for q in range(2) for k in range(2)]
    specs += [pltpu.ACC(q)((128, TB), F32) for q in range(2) for s in range(2)]
    pl.run_scoped(run, *specs)

    def post_v(n, _):
        tot = jnp.sum(sv[n].T, axis=0, keepdims=True)
        fv[n] = tot * xtv[n].astype(F32) - fv[n]
        return 0
    lax.fori_loop(0, (HALF_SHELL + 1) * NB, post_v, 0)
    total = su[0]
    for n in range(1, GT * NB):
        total = total + su[n]
    en[...] = total


def solution(mesh):
    def per_device(x_own, q_own):
        rows, feat = x_own.shape
        inv_len2 = 1.0 / feat
        grid_a, grid_t = grid_of(lax.axis_index('seg'), lax.axis_index('col'))
        sq = jnp.sum(jnp.square(x_own.astype(F32)), axis=1)
        half = -jnp.minimum(0.5 * sq, 1.7e38)
        ext = [p.reshape(8, 128) for v in (half, q_own) for p in split3(v)]
        block = jnp.concatenate([x_own] + ext, axis=0)
        axes = ('col', 'seg')
        moved = [block]
        moved += [lax.ppermute(block, axes, shift_pairs(0, d)) for d in range(1, GT)]
        moved += [lax.ppermute(block, axes, shift_pairs(d, 0)) for d in range(1, HALF_SHELL + 1)]
        xe = jnp.stack(moved)
        flags = jnp.stack([(grid_a < HALF_SHELL), (grid_t >= GT // 2)]).astype(jnp.int32)
        vm = pl.BlockSpec(memory_space=pltpu.VMEM)
        nu, nv = GT * NB, (HALF_SHELL + 1) * NB
        fu, fv, en = pl.pallas_call(
            functools.partial(pair_kernel, inv_len2 * math.log2(math.e)),
            out_shape=[jax.ShapeDtypeStruct((nu, 128, TB), F32), jax.ShapeDtypeStruct((nv, 128, TB), F32),
                       jax.ShapeDtypeStruct((8, TB), F32)],
            in_specs=[pl.BlockSpec(memory_space=pltpu.SMEM), vm],
            out_specs=[vm, vm, vm],
            scratch_shapes=[pltpu.VMEM((nu, TB, TB), BF16), pltpu.VMEM((nv, TB, TB), BF16),
                            pltpu.VMEM((nv, 128, TB), BF16), pltpu.VMEM((nu, 8, TB), F32),
                            pltpu.VMEM((nv, TB, 128), F32), pltpu.VMEM((nu, 8, TB), F32),
                            pltpu.VMEM((nv, TB, 128), F32)] + [pltpu.VMEM((TB, TB), BF16)] * 4,
            compiler_params=pltpu.CompilerParams(vmem_limit_bytes=56 * 2**20),
            name='pair_tiles',
        )(flags, xe)
        fu = fu.reshape(GT, NB, 128, TB)
        fv = fv.reshape(HALF_SHELL + 1, NB, 128, TB)
        parts = [fu[0], fv[0]]
        parts += [lax.ppermute(fu[d], axes, shift_pairs(0, -d)) for d in range(1, GT)]
        parts += [lax.ppermute(fv[d], axes, shift_pairs(-d, 0)) for d in range(1, HALF_SHELL + 1)]
        force = functools.reduce(jnp.add, parts)
        force = jnp.swapaxes(force, 1, 2).reshape(rows, feat) * inv_len2
        energy = lax.psum(jnp.sum(en), axes)
        return force, energy.reshape(1)

    row_spec = P(ROW_AXES, None)

    def step(x, q):
        with jax.sharding.use_abstract_mesh(mesh.abstract_mesh):
            return jax.shard_map(per_device, mesh=mesh, in_specs=(row_spec, P(ROW_AXES)),
                                 out_specs=(row_spec, P('sys')), check_vma=False)(x, q)
    return step
```

time: 1340 us -> 425 us (0.32)
  waiting for transfers between devices: 802 us -> 135 us
  matrix products: 403 us -> 0 us
  Pallas kernels: 0 us -> 116 us
  starting transfers between devices: 7.23 us -> 71.1 us
  loops' own time: 20.7 us -> 0 us
  local copies, waits for them, and re-layouts: 3.19 us -> 18.6 us
  between operations: 16.1 us -> 0.77 us
    ppermute x96 -> x30, waiting for transfers between devices: 768 us -> 135 us  [the longest x7 42.7 us: per_device(): lax.ppermute(block, axes, shift_pairs(0, d))]
    dot_general x98 -> x0, matrix products: 403 us -> none  [the longest x33 207 us: pair_weights(): lax.dot_general(x_host, x_vis, (((1,), (1,)), ((), ())), preferred_elemen...]
    pallas_call x0 -> x1, Pallas kernels: none -> 116 us  [per_device(): pl.pallas_call(functools.partial(pair_kernel, inv_len2 * math.log2(math.e...]
    ppermute x96 -> x30, starting transfers between devices: 7.19 us -> 71.1 us  [the longest x8 26.6 us: per_device(): lax.ppermute(fv[d], axes, shift_pairs(-d, 0))]
    reduce_scatter x1 -> x0, waiting for transfers between devices: 34 us -> none  [per_device(): lax.psum_scatter(reaction, 'col', scatter_dimension=0, tiled=True)]
    another operation x1 -> x0, loops' own time: 20.7 us -> none  [per_device(): lax.fori_loop(1, full_steps, step_body, (x_vis, q_vis, reaction, own_forc...]
  transfers between devices with their start and end apart: 97 -> 30, of which waited for: 64 -> 17; matrix products, arithmetic and copies ran while one was open for 25% -> 3% of each run, Pallas kernels for 0% -> 0%
where the time goes in v1:
time: 425 us
  waiting for transfers between devices  135 us (32%)
  Pallas kernels  116 us (27%)
  blocking collectives  75.1 us (18%)
  starting transfers between devices  71.1 us (17%)
  local copies, waits for them, and re-layouts  18.6 us (4%)
  other arithmetic  8.01 us (2%)
    pallas_call x1, Pallas kernels, per_device(): pl.pallas_call(functools.partial(pair_kernel, inv_len2 * math.log2(math.e...  116 us
    psum x1, blocking collectives, per_device(): energy = lax.psum(jnp.sum(en), axes)  75.1 us
    ppermute x7, waiting for transfers between devices, per_device(): lax.ppermute(block, axes, shift_pairs(0, d))  42.7 us
    ppermute x8, waiting for transfers between devices, per_device(): lax.ppermute(fv[d], axes, shift_pairs(-d, 0))  42.1 us
    ppermute x7, waiting for transfers between devices, per_device(): lax.ppermute(fu[d], axes, shift_pairs(0, -d))  35 us
    ppermute x8, starting transfers between devices, per_device(): lax.ppermute(fv[d], axes, shift_pairs(-d, 0))  26.6 us
    ppermute x8, starting transfers between devices, per_device(): lax.ppermute(block, axes, shift_pairs(d, 0))  26.3 us
    ppermute x8, waiting for transfers between devices, per_device(): lax.ppermute(block, axes, shift_pairs(d, 0))  15.2 us
  transfers between devices with their start and end apart: 30, of which 17 were waited for; matrix products, arithmetic and copies ran while one was open for 3% of the time, Pallas kernels for 0%

profile of v1, /device:TPU:1, one launch (start us, length us, event | category | flops | bytes accessed | tf_op | source)
XLA Modules:
  0.0 424.8 jit_solution(12390244443186083274)
XLA Ops:
  4.9 4.4 %collective-permute-start.14 = (bf16[1072,128]{1,0:T(8,128)(2,1)S(1)}, bf16[1072,128]{1,0:T(8,128)(2,1)S(1)}, u32[]{:S(2)}, u32[]{:S(2)}) collective-permute-start(bf16[1072,128]{1,0:T(8,128)(2,1)S(1)} %constant_dynamic-update-slice_fusion), channel_id=1, source_target_pairs={{32,0},{36,4},{33,1},{37,5},{34,2},{38,6},{35,3},{39,7},{96,64},{1... | collective-permute-start | bytes 823304 | tf_op jit(solution)/shard_map/ppermute | solution.py:221
  9.3 3.0 collective-permute-start.13
  12.3 2.5 collective-permute-start.12
  16.0 2.1 collective-permute-start
  19.4 3.9 collective-permute-done
  25.5 4.1 collective-permute-done.1
  29.6 4.3 %collective-permute-start.2 = (bf16[1072,128]{1,0:T(8,128)(2,1)S(1)}, bf16[1072,128]{1,0:T(8,128)(2,1)S(1)}, u32[]{:S(2)}, u32[]{:S(2)}) collective-permute-start(bf16[1072,128]{1,0:T(8,128)(2,1)S(1)} %constant_dynamic-update-slice_fusion), channel_id=1, source_target_pairs={{5,0},{2,4},{6,1},{3,5},{7,2},{0,6},{4,3},{1,7},{69,64},{66,68},{7... | collective-permute-start | bytes 823304 | tf_op jit(solution)/shard_map/ppermute | solution.py:220
  34.7 2.7 collective-permute-done.2
  37.4 2.9 collective-permute-start.3
  41.0 5.6 %collective-permute-done.3 = bf16[1072,128]{1,0:T(8,128)(2,1)S(1)} collective-permute-done((bf16[1072,128]{1,0:T(8,128)(2,1)S(1)}, bf16[1072,128]{1,0:T(8,128)(2,1)S(1)}, u32[]{:S(2)}, u32[]{:S(2)}) %collective-permute-start.3) | collective-permute-done | bytes 274464 | tf_op jit(solution)/shard_map/ppermute | solution.py:220
  48.1 8.7 %collective-permute-done.4 = bf16[1072,128]{1,0:T(8,128)(2,1)S(1)} collective-permute-done((bf16[1072,128]{1,0:T(8,128)(2,1)S(1)}, bf16[1072,128]{1,0:T(8,128)(2,1)S(1)}, u32[]{:S(2)}, u32[]{:S(2)}) %collective-permute-start.4) | collective-permute-done | bytes 274464 | tf_op jit(solution)/shard_map/ppermute | solution.py:220
  57.6 9.0 %collective-permute-done.5 = bf16[1072,128]{1,0:T(8,128)(2,1)S(1)} collective-permute-done((bf16[1072,128]{1,0:T(8,128)(2,1)S(1)}, bf16[1072,128]{1,0:T(8,128)(2,1)S(1)}, u32[]{:S(2)}, u32[]{:S(2)}) %collective-permute-start.5) | collective-permute-done | bytes 274464 | tf_op jit(solution)/shard_map/ppermute | solution.py:220
  67.3 8.7 %collective-permute-done.6 = bf16[1072,128]{1,0:T(8,128)(2,1)S(1)} collective-permute-done((bf16[1072,128]{1,0:T(8,128)(2,1)S(1)}, bf16[1072,128]{1,0:T(8,128)(2,1)S(1)}, u32[]{:S(2)}, u32[]{:S(2)}) %collective-permute-start.6) | collective-permute-done | bytes 274464 | tf_op jit(solution)/shard_map/ppermute | solution.py:220
  76.0 6.2 %collective-permute-start.7 = (bf16[1072,128]{1,0:T(8,128)(2,1)S(1)}, bf16[1072,128]{1,0:T(8,128)(2,1)S(1)}, u32[]{:S(2)}, u32[]{:S(2)}) collective-permute-start(bf16[1072,128]{1,0:T(8,128)(2,1)S(1)} %constant_dynamic-update-slice_fusion), channel_id=1, source_target_pairs={{64,0},{68,4},{65,1},{69,5},{66,2},{70,6},{67,3},{71,7},{12,64},{8... | collective-permute-start | bytes 823304 | tf_op jit(solution)/shard_map/ppermute | solution.py:221
  83.4 7.7 %collective-permute-start.8 = (bf16[1072,128]{1,0:T(8,128)(2,1)S(1)}, bf16[1072,128]{1,0:T(8,128)(2,1)S(1)}, u32[]{:S(2)}, u32[]{:S(2)}) collective-permute-start(bf16[1072,128]{1,0:T(8,128)(2,1)S(1)} %constant_dynamic-update-slice_fusion), channel_id=1, source_target_pairs={{12,0},{8,4},{13,1},{9,5},{14,2},{10,6},{15,3},{11,7},{76,64},{72,... | collective-permute-start | bytes 823304 | tf_op jit(solution)/shard_map/ppermute | solution.py:221
  91.8 4.5 %collective-permute-done.8 = bf16[1072,128]{1,0:T(8,128)(2,1)S(1)} collective-permute-done((bf16[1072,128]{1,0:T(8,128)(2,1)S(1)}, bf16[1072,128]{1,0:T(8,128)(2,1)S(1)}, u32[]{:S(2)}, u32[]{:S(2)}) %collective-permute-start.8) | collective-permute-done | bytes 274464 | tf_op jit(solution)/shard_map/ppermute | solution.py:221
  97.1 5.5 %collective-permute-done.9 = bf16[1072,128]{1,0:T(8,128)(2,1)S(1)} collective-permute-done((bf16[1072,128]{1,0:T(8,128)(2,1)S(1)}, bf16[1072,128]{1,0:T(8,128)(2,1)S(1)}, u32[]{:S(2)}, u32[]{:S(2)}) %collective-permute-start.9) | collective-permute-done | bytes 274464 | tf_op jit(solution)/shard_map/ppermute | solution.py:221
  104.6 4.7 %collective-permute-done.10 = bf16[1072,128]{1,0:T(8,128)(2,1)S(1)} collective-permute-done((bf16[1072,128]{1,0:T(8,128)(2,1)S(1)}, bf16[1072,128]{1,0:T(8,128)(2,1)S(1)}, u32[]{:S(2)}, u32[]{:S(2)}) %collective-permute-start.10) | collective-permute-done | bytes 274464 | tf_op jit(solution)/shard_map/ppermute | solution.py:221
  113.1 116.3 %pair_tiles.1 = (f32[32,128,256]{2,1,0:T(8,128)}, f32[36,128,256]{2,1,0:T(8,128)}, f32[8,256]{1,0:T(8,128)}) custom-call(s32[2]{0:T(128)} %add_convert_fusion.flags, bf16[16,1072,128]{2,1,0:T(8,128)(2,1)} %bitcast_dynamic-update-slice_fusion.xe), custom_call_target="tpu_custom_call" | custom-call | tf_op jit(solution)/shard_map/pair_tiles/pallas_call | solution.py:226
  229.3 2.4 fusion.8
  231.8 1.9 collective-permute-start.15
  236.6 1.8 collective-permute-start.18
  240.0 24.9 %collective-permute-done.15 = f32[4,128,256]{2,1,0:T(8,128)S(1)} collective-permute-done((f32[4,128,256]{2,1,0:T(8,128)S(1)}, f32[4,128,256]{2,1,0:T(8,128)S(1)}, u32[]{:S(2)}, u32[]{:S(2)}) %collective-permute-start.15) | collective-permute-done | bytes 524320 | tf_op jit(solution)/shard_map/ppermute | solution.py:242
  264.9 4.3 %collective-permute-done.21 = f32[4,128,256]{2,1,0:T(8,128)S(1)} collective-permute-done((f32[4,128,256]{2,1,0:T(8,128)S(1)}, f32[4,128,256]{2,1,0:T(8,128)S(1)}, u32[]{:S(2)}, u32[]{:S(2)}) %collective-permute-start.21) | collective-permute-done | bytes 524320 | tf_op jit(solution)/shard_map/ppermute | solution.py:242
  269.2 6.2 %collective-permute-start.22 = (f32[4,128,256]{2,1,0:T(8,128)S(1)}, f32[4,128,256]{2,1,0:T(8,128)S(1)}, u32[]{:S(2)}, u32[]{:S(2)}) collective-permute-start(f32[4,128,256]{2,1,0:T(8,128)S(1)} %get-tuple-element.8), channel_id=1, source_target_pairs={{124,0},{120,4},{125,1},{121,5},{126,2},{122,6},{127,3},{123,7},{0... | collective-permute-start | bytes 1572872 | tf_op jit(solution)/shard_map/ppermute | solution.py:243
  275.6 4.3 %collective-permute-done.17 = f32[4,128,256]{2,1,0:T(8,128)S(1)} collective-permute-done((f32[4,128,256]{2,1,0:T(8,128)S(1)}, f32[4,128,256]{2,1,0:T(8,128)S(1)}, u32[]{:S(2)}, u32[]{:S(2)}) %collective-permute-start.17) | collective-permute-done | bytes 524320 | tf_op jit(solution)/shard_map/ppermute | solution.py:242
  279.9 9.8 %collective-permute-start.27 = (f32[4,128,256]{2,1,0:T(8,128)}, f32[4,128,256]{2,1,0:T(8,128)}, u32[]{:S(2)}, u32[]{:S(2)}) collective-permute-start(f32[4,128,256]{2,1,0:T(8,128)} %get-tuple-element.11), channel_id=1, source_target_pairs={{44,0},{40,4},{45,1},{41,5},{46,2},{42,6},{47,3},{43,7},{108,64},{... | collective-permute-start | bytes 1572872 | tf_op jit(solution)/shard_map/ppermute | solution.py:243
  291.2 10.4 %collective-permute-start.26 = (f32[4,128,256]{2,1,0:T(8,128)}, f32[4,128,256]{2,1,0:T(8,128)}, u32[]{:S(2)}, u32[]{:S(2)}) collective-permute-start(f32[4,128,256]{2,1,0:T(8,128)} %get-tuple-element.12), channel_id=1, source_target_pairs={{108,0},{104,4},{109,1},{105,5},{110,2},{106,6},{111,3},{107,7},{4... | collective-permute-start | bytes 1572872 | tf_op jit(solution)/shard_map/ppermute | solution.py:243
  301.6 20.9 %collective-permute-done.29 = f32[4,128,256]{2,1,0:T(8,128)S(1)} collective-permute-done((f32[4,128,256]{2,1,0:T(8,128)S(1)}, f32[4,128,256]{2,1,0:T(8,128)S(1)}, u32[]{:S(2)}, u32[]{:S(2)}) %collective-permute-start.29) | collective-permute-done | bytes 524320 | tf_op jit(solution)/shard_map/ppermute | solution.py:243
  322.5 21.2 %collective-permute-done.28 = f32[4,128,256]{2,1,0:T(8,128)S(1)} collective-permute-done((f32[4,128,256]{2,1,0:T(8,128)S(1)}, f32[4,128,256]{2,1,0:T(8,128)S(1)}, u32[]{:S(2)}, u32[]{:S(2)}) %collective-permute-start.28) | collective-permute-done | bytes 524320 | tf_op jit(solution)/shard_map/ppermute | solution.py:243
  345.1 75.1 %psum.7 = f32[1]{0:T(128)} all-reduce(f32[1]{0:T(128)} %bitcast.24), channel_id=1, replica_groups=mesh['sys'=1,'col'=2,'seg'=64] {'col','seg'}, use_global_device_ids=true, to_apply=%region_2.3 | all-reduce | flops 1 | bytes 8 | tf_op jit(solution)/shard_map/psum | solution.py:246
  420.2 3.5 multiply_bitcast_fusion
  (74 shorter events, 30.4 us)
Async XLA Ops:
  4.9 107.4 %collective-permute-start.14 = (bf16[1072,128]{1,0:T(8,128)(2,1)S(1)}, bf16[1072,128]{1,0:T(8,128)(2,1)S(1)}, u32[]{:S(2)}, u32[]{:S(2)}) collective-permute-start(bf16[1072,128]{1,0:T(8,128)(2,1)S(1)} %constant_dynamic-update-slice_fusion), channel_id=1, source_target_pairs={{32,0},{36,4},{33,1},{37,5},{34,2},{38,6},{35,3},{39,7},{96,64},{1... | collective-permute-start | bytes 823304 | tf_op jit(solution)/shard_map/ppermute | solution.py:221
  9.3 102.3 %collective-permute-start.13 = (bf16[1072,128]{1,0:T(8,128)(2,1)S(1)}, bf16[1072,128]{1,0:T(8,128)(2,1)S(1)}, u32[]{:S(2)}, u32[]{:S(2)}) collective-permute-start(bf16[1072,128]{1,0:T(8,128)(2,1)S(1)} %constant_dynamic-update-slice_fusion), channel_id=1, source_target_pairs={{92,0},{88,4},{93,1},{89,5},{94,2},{90,6},{95,3},{91,7},{32,64},{3... | collective-permute-start | bytes 823304 | tf_op jit(solution)/shard_map/ppermute | solution.py:221
  12.3 98.5 %collective-permute-start.12 = (bf16[1072,128]{1,0:T(8,128)(2,1)S(1)}, bf16[1072,128]{1,0:T(8,128)(2,1)S(1)}, u32[]{:S(2)}, u32[]{:S(2)}) collective-permute-start(bf16[1072,128]{1,0:T(8,128)(2,1)S(1)} %constant_dynamic-update-slice_fusion), channel_id=1, source_target_pairs={{28,0},{24,4},{29,1},{25,5},{30,2},{26,6},{31,3},{27,7},{92,64},{8... | collective-permute-start | bytes 823304 | tf_op jit(solution)/shard_map/ppermute | solution.py:221
  14.8 95.3 %collective-permute-start.11 = (bf16[1072,128]{1,0:T(8,128)(2,1)S(1)}, bf16[1072,128]{1,0:T(8,128)(2,1)S(1)}, u32[]{:S(2)}, u32[]{:S(2)}) collective-permute-start(bf16[1072,128]{1,0:T(8,128)(2,1)S(1)} %constant_dynamic-update-slice_fusion), channel_id=1, source_target_pairs={{80,0},{84,4},{81,1},{85,5},{82,2},{86,6},{83,3},{87,7},{28,64},{2... | collective-permute-start | bytes 823304 | tf_op jit(solution)/shard_map/ppermute | solution.py:221
  16.0 7.3 %collective-permute-start = (bf16[1072,128]{1,0:T(8,128)(2,1)S(1)}, bf16[1072,128]{1,0:T(8,128)(2,1)S(1)}, u32[]{:S(2)}, u32[]{:S(2)}) collective-permute-start(bf16[1072,128]{1,0:T(8,128)(2,1)S(1)} %constant_dynamic-update-slice_fusion), channel_id=1, source_target_pairs={{4,0},{1,4},{5,1},{2,5},{6,2},{3,6},{7,3},{0,7},{68,64},{65,68},{6... | collective-permute-start | bytes 823304 | tf_op jit(solution)/shard_map/ppermute | solution.py:220
  23.3 6.3 %collective-permute-start.1 = (bf16[1072,128]{1,0:T(8,128)(2,1)S(1)}, bf16[1072,128]{1,0:T(8,128)(2,1)S(1)}, u32[]{:S(2)}, u32[]{:S(2)}) collective-permute-start(bf16[1072,128]{1,0:T(8,128)(2,1)S(1)} %constant_dynamic-update-slice_fusion), channel_id=1, source_target_pairs={{1,0},{5,4},{2,1},{6,5},{3,2},{7,6},{0,3},{4,7},{65,64},{69,68},{6... | collective-permute-start | bytes 823304 | tf_op jit(solution)/shard_map/ppermute | solution.py:220
  29.6 7.8 %collective-permute-start.2 = (bf16[1072,128]{1,0:T(8,128)(2,1)S(1)}, bf16[1072,128]{1,0:T(8,128)(2,1)S(1)}, u32[]{:S(2)}, u32[]{:S(2)}) collective-permute-start(bf16[1072,128]{1,0:T(8,128)(2,1)S(1)} %constant_dynamic-update-slice_fusion), channel_id=1, source_target_pairs={{5,0},{2,4},{6,1},{3,5},{7,2},{0,6},{4,3},{1,7},{69,64},{66,68},{7... | collective-permute-start | bytes 823304 | tf_op jit(solution)/shard_map/ppermute | solution.py:220
  37.4 9.2 %collective-permute-start.3 = (bf16[1072,128]{1,0:T(8,128)(2,1)S(1)}, bf16[1072,128]{1,0:T(8,128)(2,1)S(1)}, u32[]{:S(2)}, u32[]{:S(2)}) collective-permute-start(bf16[1072,128]{1,0:T(8,128)(2,1)S(1)} %constant_dynamic-update-slice_fusion), channel_id=1, source_target_pairs={{2,0},{6,4},{3,1},{7,5},{0,2},{4,6},{1,3},{5,7},{66,64},{70,68},{6... | collective-permute-start | bytes 823304 | tf_op jit(solution)/shard_map/ppermute | solution.py:220
  46.6 10.3 %collective-permute-start.4 = (bf16[1072,128]{1,0:T(8,128)(2,1)S(1)}, bf16[1072,128]{1,0:T(8,128)(2,1)S(1)}, u32[]{:S(2)}, u32[]{:S(2)}) collective-permute-start(bf16[1072,128]{1,0:T(8,128)(2,1)S(1)} %constant_dynamic-update-slice_fusion), channel_id=1, source_target_pairs={{6,0},{3,4},{7,1},{0,5},{4,2},{1,6},{5,3},{2,7},{70,64},{67,68},{7... | collective-permute-start | bytes 823304 | tf_op jit(solution)/shard_map/ppermute | solution.py:220
  56.9 9.7 %collective-permute-start.5 = (bf16[1072,128]{1,0:T(8,128)(2,1)S(1)}, bf16[1072,128]{1,0:T(8,128)(2,1)S(1)}, u32[]{:S(2)}, u32[]{:S(2)}) collective-permute-start(bf16[1072,128]{1,0:T(8,128)(2,1)S(1)} %constant_dynamic-update-slice_fusion), channel_id=1, source_target_pairs={{3,0},{7,4},{0,1},{4,5},{1,2},{5,6},{2,3},{6,7},{67,64},{71,68},{6... | collective-permute-start | bytes 823304 | tf_op jit(solution)/shard_map/ppermute | solution.py:220
  66.6 9.4 %collective-permute-start.6 = (bf16[1072,128]{1,0:T(8,128)(2,1)S(1)}, bf16[1072,128]{1,0:T(8,128)(2,1)S(1)}, u32[]{:S(2)}, u32[]{:S(2)}) collective-permute-start(bf16[1072,128]{1,0:T(8,128)(2,1)S(1)} %constant_dynamic-update-slice_fusion), channel_id=1, source_target_pairs={{7,0},{0,4},{4,1},{1,5},{5,2},{2,6},{6,3},{3,7},{71,64},{64,68},{6... | collective-permute-start | bytes 823304 | tf_op jit(solution)/shard_map/ppermute | solution.py:220
  76.0 7.4 %collective-permute-start.7 = (bf16[1072,128]{1,0:T(8,128)(2,1)S(1)}, bf16[1072,128]{1,0:T(8,128)(2,1)S(1)}, u32[]{:S(2)}, u32[]{:S(2)}) collective-permute-start(bf16[1072,128]{1,0:T(8,128)(2,1)S(1)} %constant_dynamic-update-slice_fusion), channel_id=1, source_target_pairs={{64,0},{68,4},{65,1},{69,5},{66,2},{70,6},{67,3},{71,7},{12,64},{8... | collective-permute-start | bytes 823304 | tf_op jit(solution)/shard_map/ppermute | solution.py:221
  83.4 12.9 %collective-permute-start.8 = (bf16[1072,128]{1,0:T(8,128)(2,1)S(1)}, bf16[1072,128]{1,0:T(8,128)(2,1)S(1)}, u32[]{:S(2)}, u32[]{:S(2)}) collective-permute-start(bf16[1072,128]{1,0:T(8,128)(2,1)S(1)} %constant_dynamic-update-slice_fusion), channel_id=1, source_target_pairs={{12,0},{8,4},{13,1},{9,5},{14,2},{10,6},{15,3},{11,7},{76,64},{72,... | collective-permute-start | bytes 823304 | tf_op jit(solution)/shard_map/ppermute | solution.py:221
  96.4 6.2 %collective-permute-start.9 = (bf16[1072,128]{1,0:T(8,128)(2,1)S(1)}, bf16[1072,128]{1,0:T(8,128)(2,1)S(1)}, u32[]{:S(2)}, u32[]{:S(2)}) collective-permute-start(bf16[1072,128]{1,0:T(8,128)(2,1)S(1)} %constant_dynamic-update-slice_fusion), channel_id=1, source_target_pairs={{76,0},{72,4},{77,1},{73,5},{78,2},{74,6},{79,3},{75,7},{16,64},{2... | collective-permute-start | bytes 823304 | tf_op jit(solution)/shard_map/ppermute | solution.py:221
  102.6 6.7 %collective-permute-start.10 = (bf16[1072,128]{1,0:T(8,128)(2,1)S(1)}, bf16[1072,128]{1,0:T(8,128)(2,1)S(1)}, u32[]{:S(2)}, u32[]{:S(2)}) collective-permute-start(bf16[1072,128]{1,0:T(8,128)(2,1)S(1)} %constant_dynamic-update-slice_fusion), channel_id=1, source_target_pairs={{16,0},{20,4},{17,1},{21,5},{18,2},{22,6},{19,3},{23,7},{80,64},{8... | collective-permute-start | bytes 823304 | tf_op jit(solution)/shard_map/ppermute | solution.py:221
  231.8 112.7 %copy-start.6 = (f32[8,256]{1,0:T(8,128)S(1)}, f32[8,256]{1,0:T(8,128)}, u32[]{:S(2)}) copy-start(f32[8,256]{1,0:T(8,128)} %get-tuple-element.7) | copy-start | bytes 24580
  231.8 33.1 %collective-permute-start.15 = (f32[4,128,256]{2,1,0:T(8,128)S(1)}, f32[4,128,256]{2,1,0:T(8,128)S(1)}, u32[]{:S(2)}, u32[]{:S(2)}) collective-permute-start(f32[4,128,256]{2,1,0:T(8,128)S(1)} %get-tuple-element.16), channel_id=1, source_target_pairs={{7,0},{0,4},{4,1},{1,5},{5,2},{2,6},{6,3},{3,7},{71,64},{64,68},{6... | collective-permute-start | bytes 1572872 | tf_op jit(solution)/shard_map/ppermute | solution.py:242
  233.7 35.6 %collective-permute-start.21 = (f32[4,128,256]{2,1,0:T(8,128)S(1)}, f32[4,128,256]{2,1,0:T(8,128)S(1)}, u32[]{:S(2)}, u32[]{:S(2)}) collective-permute-start(f32[4,128,256]{2,1,0:T(8,128)S(1)} %get-tuple-element.17), channel_id=1, source_target_pairs={{4,0},{1,4},{5,1},{2,5},{6,2},{3,6},{7,3},{0,7},{68,64},{65,68},{6... | collective-permute-start | bytes 1572872 | tf_op jit(solution)/shard_map/ppermute | solution.py:242
  235.4 33.8 %collective-permute-start.20 = (f32[4,128,256]{2,1,0:T(8,128)S(1)}, f32[4,128,256]{2,1,0:T(8,128)S(1)}, u32[]{:S(2)}, u32[]{:S(2)}) collective-permute-start(f32[4,128,256]{2,1,0:T(8,128)S(1)} %get-tuple-element.18), channel_id=1, source_target_pairs={{1,0},{5,4},{2,1},{6,5},{3,2},{7,6},{0,3},{4,7},{65,64},{69,68},{6... | collective-permute-start | bytes 1572872 | tf_op jit(solution)/shard_map/ppermute | solution.py:242
  235.4 40.0 %collective-permute-start.19 = (f32[4,128,256]{2,1,0:T(8,128)S(1)}, f32[4,128,256]{2,1,0:T(8,128)S(1)}, u32[]{:S(2)}, u32[]{:S(2)}) collective-permute-start(f32[4,128,256]{2,1,0:T(8,128)S(1)} %get-tuple-element.19), channel_id=1, source_target_pairs={{5,0},{2,4},{6,1},{3,5},{7,2},{0,6},{4,3},{1,7},{69,64},{66,68},{7... | collective-permute-start | bytes 1572872 | tf_op jit(solution)/shard_map/ppermute | solution.py:242
  236.6 39.0 %collective-permute-start.18 = (f32[4,128,256]{2,1,0:T(8,128)S(1)}, f32[4,128,256]{2,1,0:T(8,128)S(1)}, u32[]{:S(2)}, u32[]{:S(2)}) collective-permute-start(f32[4,128,256]{2,1,0:T(8,128)S(1)} %get-tuple-element.20), channel_id=1, source_target_pairs={{2,0},{6,4},{3,1},{7,5},{0,2},{4,6},{1,3},{5,7},{66,64},{70,68},{6... | collective-permute-start | bytes 1572872 | tf_op jit(solution)/shard_map/ppermute | solution.py:242
  264.9 15.0 %collective-permute-start.17 = (f32[4,128,256]{2,1,0:T(8,128)S(1)}, f32[4,128,256]{2,1,0:T(8,128)S(1)}, u32[]{:S(2)}, u32[]{:S(2)}) collective-permute-start(f32[4,128,256]{2,1,0:T(8,128)S(1)} %get-tuple-element.21), channel_id=1, source_target_pairs={{6,0},{3,4},{7,1},{0,5},{4,2},{1,6},{5,3},{2,7},{70,64},{67,68},{7... | collective-permute-start | bytes 1572872 | tf_op jit(solution)/shard_map/ppermute | solution.py:242
  269.2 21.9 %collective-permute-start.16 = (f32[4,128,256]{2,1,0:T(8,128)S(1)}, f32[4,128,256]{2,1,0:T(8,128)S(1)}, u32[]{:S(2)}, u32[]{:S(2)}) collective-permute-start(f32[4,128,256]{2,1,0:T(8,128)S(1)} %get-tuple-element.22), channel_id=1, source_target_pairs={{3,0},{7,4},{0,1},{4,5},{1,2},{5,6},{2,3},{6,7},{67,64},{71,68},{6... | collective-permute-start | bytes 1572872 | tf_op jit(solution)/shard_map/ppermute | solution.py:242
  269.2 32.3 %collective-permute-start.22 = (f32[4,128,256]{2,1,0:T(8,128)S(1)}, f32[4,128,256]{2,1,0:T(8,128)S(1)}, u32[]{:S(2)}, u32[]{:S(2)}) collective-permute-start(f32[4,128,256]{2,1,0:T(8,128)S(1)} %get-tuple-element.8), channel_id=1, source_target_pairs={{124,0},{120,4},{125,1},{121,5},{126,2},{122,6},{127,3},{123,7},{0... | collective-permute-start | bytes 1572872 | tf_op jit(solution)/shard_map/ppermute | solution.py:243
  275.5 47.0 %collective-permute-start.29 = (f32[4,128,256]{2,1,0:T(8,128)S(1)}, f32[4,128,256]{2,1,0:T(8,128)S(1)}, u32[]{:S(2)}, u32[]{:S(2)}) collective-permute-start(f32[4,128,256]{2,1,0:T(8,128)S(1)} %get-tuple-element.9), channel_id=1, source_target_pairs={{32,0},{36,4},{33,1},{37,5},{34,2},{38,6},{35,3},{39,7},{96,64},{1... | collective-permute-start | bytes 1572872 | tf_op jit(solution)/shard_map/ppermute | solution.py:243
  275.6 68.1 %collective-permute-start.28 = (f32[4,128,256]{2,1,0:T(8,128)S(1)}, f32[4,128,256]{2,1,0:T(8,128)S(1)}, u32[]{:S(2)}, u32[]{:S(2)}) collective-permute-start(f32[4,128,256]{2,1,0:T(8,128)S(1)} %get-tuple-element.10), channel_id=1, source_target_pairs={{96,0},{100,4},{97,1},{101,5},{98,2},{102,6},{99,3},{103,7},{44,64... | collective-permute-start | bytes 1572872 | tf_op jit(solution)/shard_map/ppermute | solution.py:243
  279.9 140.3 %collective-permute-start.27 = (f32[4,128,256]{2,1,0:T(8,128)}, f32[4,128,256]{2,1,0:T(8,128)}, u32[]{:S(2)}, u32[]{:S(2)}) collective-permute-start(f32[4,128,256]{2,1,0:T(8,128)} %get-tuple-element.11), channel_id=1, source_target_pairs={{44,0},{40,4},{45,1},{41,5},{46,2},{42,6},{47,3},{43,7},{108,64},{... | collective-permute-start | bytes 1572872 | tf_op jit(solution)/shard_map/ppermute | solution.py:243
  291.2 52.5 %copy-start.2 = (f32[4,128,256]{2,1,0:T(8,128)}, f32[4,128,256]{2,1,0:T(8,128)S(1)}, u32[]{:S(2)}) copy-start(f32[4,128,256]{2,1,0:T(8,128)S(1)} %collective-permute-done.16) | copy-start | bytes 1572868
  291.2 129.0 %collective-permute-start.26 = (f32[4,128,256]{2,1,0:T(8,128)}, f32[4,128,256]{2,1,0:T(8,128)}, u32[]{:S(2)}, u32[]{:S(2)}) collective-permute-start(f32[4,128,256]{2,1,0:T(8,128)} %get-tuple-element.12), channel_id=1, source_target_pairs={{108,0},{104,4},{109,1},{105,5},{110,2},{106,6},{111,3},{107,7},{4... | collective-permute-start | bytes 1572872 | tf_op jit(solution)/shard_map/ppermute | solution.py:243
  301.6 118.6 %collective-permute-start.25 = (f32[4,128,256]{2,1,0:T(8,128)}, f32[4,128,256]{2,1,0:T(8,128)}, u32[]{:S(2)}, u32[]{:S(2)}) collective-permute-start(f32[4,128,256]{2,1,0:T(8,128)} %get-tuple-element.13), channel_id=1, source_target_pairs={{48,0},{52,4},{49,1},{53,5},{50,2},{54,6},{51,3},{55,7},{112,64},{... | collective-permute-start | bytes 1572872 | tf_op jit(solution)/shard_map/ppermute | solution.py:243
  322.5 97.8 %collective-permute-start.24 = (f32[4,128,256]{2,1,0:T(8,128)}, f32[4,128,256]{2,1,0:T(8,128)}, u32[]{:S(2)}, u32[]{:S(2)}) collective-permute-start(f32[4,128,256]{2,1,0:T(8,128)} %get-tuple-element.14), channel_id=1, source_target_pairs={{112,0},{116,4},{113,1},{117,5},{114,2},{118,6},{115,3},{119,7},{6... | collective-permute-start | bytes 1572872 | tf_op jit(solution)/shard_map/ppermute | solution.py:243
  343.7 76.5 %collective-permute-start.23 = (f32[4,128,256]{2,1,0:T(8,128)S(1)}, f32[4,128,256]{2,1,0:T(8,128)}, u32[]{:S(2)}, u32[]{:S(2)}) collective-permute-start(f32[4,128,256]{2,1,0:T(8,128)S(1)} %get-tuple-element.15), channel_id=1, source_target_pairs={{60,0},{56,4},{61,1},{57,5},{62,2},{58,6},{63,3},{59,7},{124,64},{... | collective-permute-start | bytes 1572872 | tf_op jit(solution)/shard_map/ppermute | solution.py:243
  (5 other events, 84.5 us)

commit v2 on v1

v2 whole, which is shorter than its diff:
```python
import functools
import math

import jax
import jax.numpy as jnp
from jax import lax
from jax.experimental import pallas as pl
from jax.experimental.pallas import tpu as pltpu
from jax.sharding import PartitionSpec as P

F32 = jnp.float32
BF16 = jnp.bfloat16
ROW_AXES = ('sys', 'seg', 'col')
GA, GT = 16, 8
OWN = 1024
TB = 256
NB = OWN // TB
EXT = 48
PR = 64
NP = TB // PR
HALF = GA // 2
HOST_STEP = (0, 1, 7, 4, 3, 5, 6, 2)
EITHER = -1
MESH = pl.DeviceIdType.MESH

UNITS = [(u, v) for u in range(GT) for v in range(1, HALF)]
UNITS += [(HOST_STEP.index(d), v) for d in (1, 2, 3) for v in (0, HALF)]
UNITS += [(HOST_STEP.index(4), EITHER), (0, HALF)]
UNITS.sort(key=lambda pair: pair[0])
ONCE = (0, HALF)


def grid_of(seg, col):
    z, y, x = seg // 16, (seg // 4) % 4, seg % 4
    ya = y // 2
    yb = (ya + y % 2) % 2
    return (z * 2 + ya) * 2 + col, x * 2 + yb


def device_at(a, t):
    ya, yb = (a // 2) % 2, t % 2
    return {'seg': (a // 4) * 16 + (2 * ya + (ya + yb) % 2) * 4 + t // 2, 'col': a % 2}


def split3(v):
    hi = lax.reduce_precision(v, 8, 7)
    mid = lax.reduce_precision(v - hi, 8, 7)
    lo = lax.reduce_precision(v - hi - mid, 8, 7)
    return [p.astype(BF16) for p in (hi, mid, lo)]


def pick(table, n):
    out = jnp.int32(table[0])
    for k in range(1, len(table)):
        if table[k] != table[k - 1]:
            out = jnp.where(n >= k, table[k], out)
    return out


class Ring:
    def __init__(self):
        self.a, self.t = grid_of(lax.axis_index('seg'), lax.axis_index('col'))

    def peer(self, da, dt):
        return device_at((self.a + da + GA) % GA, (self.t + dt + GT) % GT)

    def enter(self):
        barrier = pltpu.get_barrier_semaphore()
        for d in range(1, GT):
            pl.semaphore_signal(barrier, inc=1, device_id=self.peer(0, d), device_id_type=MESH)
        for d in range(1, GA):
            pl.semaphore_signal(barrier, inc=1, device_id=self.peer(d, 0), device_id_type=MESH)
        pl.semaphore_wait(barrier, GT + GA - 2)


def gather_kernel(blk, xe, own, snd, rcv):
    ring = Ring()
    keep = pltpu.make_async_copy(blk, xe.at[0], own)
    keep.start()
    ring.enter()
    copies = []
    for n in range(1, HALF + 1):
        for slot in ([GT - 1 + n, n] if n < GT else [GT - 1 + n]):
            to = ring.peer(0, -HOST_STEP[slot]) if slot < GT else ring.peer(-(slot - GT + 1), 0)
            copies.append(pltpu.make_async_remote_copy(src_ref=blk, dst_ref=xe.at[slot], send_sem=snd.at[slot],
                                                       recv_sem=rcv.at[slot], device_id=to, device_id_type=MESH))
            copies[-1].start()
    keep.wait()
    for copy in copies:
        copy.wait_recv()
    for copy in copies:
        copy.wait_send()


def reduce_kernel(inv_len2, fu, fv, en, force_out, en_out, rb, er, ec, mine, own, fsnd, frcv, esnd, ercv):
    ring = Ring()
    keep = [pltpu.make_async_copy(f.at[pl.ds(0, NB)], mine.at[n], own.at[n]) for n, f in enumerate((fu, fv))]
    for copy in keep:
        copy.start()
    ring.enter()
    copies = []
    for n in range(1, HALF + 1):
        for slot in ([GT - 1 + n, n] if n < GT else [GT - 1 + n]):
            src = fu.at[pl.ds(NB * slot, NB)] if slot < GT else fv.at[pl.ds(NB * (slot - GT + 1), NB)]
            to = ring.peer(0, HOST_STEP[slot]) if slot < GT else ring.peer(slot - GT + 1, 0)
            copies.append(pltpu.make_async_remote_copy(src_ref=src, dst_ref=rb.at[slot - 1], send_sem=fsnd.at[slot],
                                                       recv_sem=frcv.at[slot], device_id=to, device_id_type=MESH))
            copies[-1].start()

    def spread(ref, me, along_t):
        out = []
        for n in range(1, GT if along_t else GA):
            k = n if along_t else GT + n
            out.append(pltpu.make_async_remote_copy(src_ref=ref.at[me], dst_ref=ref.at[me], send_sem=esnd.at[k],
                                                    recv_sem=ercv.at[k], device_id=ring.peer(0, n) if along_t else ring.peer(n, 0),
                                                    device_id_type=MESH))
        for copy in out:
            copy.start()
        return out

    def fold(r, count):
        total = r[0]
        for n in range(1, count):
            total = total + r[n]
        return total

    er[ring.t] = en[...]
    for copy in keep:
        copy.wait()
    along = spread(er, ring.t, True)
    for copy in along:
        copy.wait_recv()
    ec[ring.a] = fold(er, GT)
    copies[0].wait_recv()
    across = spread(ec, ring.a, False)
    for copy in copies[1:]:
        copy.wait_recv()
    for copy in across:
        copy.wait_recv()
    en_out[...] = fold(ec, GA)

    def all_sum(ib, _):
        out = mine[0, ib] + mine[1, ib]
        for slot in range(GT + HALF - 1):
            out = out + rb[slot, ib]
        force_out[pl.ds(pl.multiple_of(ib * TB, TB), TB), :] = (out * inv_len2).T
        return 0
    lax.fori_loop(0, NB, all_sum, 0)
    for copy in copies + along + across:
        copy.wait_send()


def pair_kernel(scale, place, xe, fu, fv, en, xi, xv, xtv, qu, qv, su, sv, *wsc):
    my_a, my_t = place[0], place[1]
    def ext_row(b, m, ib):
        row = xe[b, OWN + 8 * m:OWN + 8 * (m + 1), :].astype(F32)
        sel = lax.broadcasted_iota(jnp.int32, (8, 128), 0)
        lo = jnp.sum(jnp.where(sel == 2 * ib, row, 0.0), axis=0, keepdims=True)
        hi = jnp.sum(jnp.where(sel == 2 * ib + 1, row, 0.0), axis=0, keepdims=True)
        return jnp.concatenate([lo, hi], axis=1)

    def aug_rows(b, ib, s_first):
        r = lax.broadcasted_iota(jnp.int32, (128, TB), 0)
        out = jnp.where((r >= 3 - s_first) & (r < 6 - s_first), 1.0, 0.0)
        for m in range(3):
            out = jnp.where(r == s_first + m, ext_row(b, m, ib), out)
        return out.astype(BF16)

    def charge_row(b, ib):
        return (ext_row(b, 3, ib) + ext_row(b, 4, ib)) + ext_row(b, 5, ib)

    def prep_u(u):
        def one(ib, _):
            n = u * NB + ib
            xi[n, 0:128, :] = xe[u, pl.ds(pl.multiple_of(ib * TB, TB), TB), :].T
            xi[n, 128:256, :] = aug_rows(u, ib, 3)
            qu[n] = jnp.broadcast_to(charge_row(u, ib), (8, TB))
            su[n] = jnp.zeros((8, TB), F32)
            fu[n] = jnp.zeros((128, TB), F32)
            return 0
        lax.fori_loop(0, NB, one, 0)

    def prep_v(v):
        b = GT - 1 + v if v else 0

        def one(ib, _):
            n = v * NB + ib
            xb = xe[b, pl.ds(pl.multiple_of(ib * TB, TB), TB), :]
            xv[n, :, 0:128] = xb
            xv[n, :, 128:256] = aug_rows(b, ib, 0).T
            xtv[n] = xb.T
            qv[n] = jnp.broadcast_to(charge_row(b, ib), (128, TB)).T
            sv[n] = jnp.zeros((TB, 128), F32)
            fv[n] = jnp.zeros((128, TB), F32)
            return 0
        lax.fori_loop(0, NB, one, 0)

    for n in range(GT):
        prep_u(n)
    for n in range(HALF + 1):
        prep_v(n)


    def finish_u(u):
        def one(ib, _):
            n = u * NB + ib
            fu[n] = jnp.sum(su[n], axis=0, keepdims=True) * xi[n, 0:128, :].astype(F32) - fu[n]
            return 0
        lax.fori_loop(0, NB, one, 0)

    def finish_v(v):
        def one(ib, _):
            n = v * NB + ib
            fv[n] = jnp.sum(sv[n].T, axis=0, keepdims=True) * xtv[n].astype(F32) - fv[n]
            return 0
        lax.fori_loop(0, NB, one, 0)

    def run(*accs):
        G = lambda q, k, p: accs[(q * 2 + k) * NP + p]
        F = lambda q, k: accs[4 * NP + q * 2 + k]
        FJ = lambda q, s: accs[4 * NP + 4 + q * 2 + s]

        def issue_g(u, bj, k):
            for q in range(2):
                pltpu.matmul_push_rhs(xi[NB * u + 2 * k + q], staging_register=1, mxu_index=q)
            for p in range(NP):
                lhs = xv[bj, p * PR:(p + 1) * PR, :]
                for q in range(2):
                    pltpu.matmul_acc_lhs(G(q, k, p), lhs, load_staged_rhs=1 if p == 0 else None)

        def elem(u, bj, k, weight, masked):
            cs = [None, None]
            for p in range(NP):
                qvr = qv[bj, p * PR:(p + 1) * PR, :]
                rs = None
                for q in range(2):
                    ib = NB * u + 2 * k + q
                    quv = qu[ib, 0:1, :] * weight
                    g = pltpu.matmul_pop(G(q, k, p))
                    e = jnp.exp2(jnp.minimum(g * scale, 0.0))
                    w0 = (qvr * quv[:, :128]) * e[:, :128]
                    w1 = (qvr * quv[:, 128:]) * e[:, 128:]
                    w = jnp.concatenate([w0, w1], axis=1)
                    if masked:
                        jj = bj * TB + p * PR + lax.broadcasted_iota(jnp.int32, (PR, TB), 0)
                        ii = ib * TB + lax.broadcasted_iota(jnp.int32, (PR, TB), 1)
                        w = jnp.where(jj < ii, w, 0.0)
                        w0, w1 = w[:, :128], w[:, 128:]
                    wsc[q * 2 + k][p * PR:(p + 1) * PR, :] = w.astype(BF16)
                    c = jnp.sum(w.reshape(PR // 8, 8, TB), axis=0)
                    cs[q] = c if cs[q] is None else cs[q] + c
                    rs = w0 + w1 if rs is None else rs + (w0 + w1)
                sv[bj, p * PR:(p + 1) * PR, :] += rs
            for q in range(2):
                su[NB * u + 2 * k + q] += cs[q]

        def force(u, bj, k, s):
            for q in range(2):
                pltpu.matmul_push_rhs(wsc[q * 2 + k][...], staging_register=1, mxu_index=q)
            lhs = xtv[bj]
            for q in range(2):
                pltpu.matmul_acc_lhs(F(q, k), lhs, load_staged_rhs=1)
            for q in range(2):
                pltpu.matmul_push_rhs(wsc[q * 2 + k][...], staging_register=0, mxu_index=q, transpose=True)
            for q in range(2):
                pltpu.matmul_acc_lhs(FJ(q, s), xi[NB * u + 2 * k + q, 0:128, :], load_staged_rhs=0)

        def flush(bj, s):
            fv[bj] += pltpu.matmul_pop(FJ(0, s)) + pltpu.matmul_pop(FJ(1, s))

        def host_pop(u, k):
            for q in range(2):
                fu[NB * u + 2 * k + q] += pltpu.matmul_pop(F(q, k))

        def unit(prev, cur, nxt, masked):
            weight = 1.0 if masked else jnp.where((cur[0] == ONCE[0]) & (cur[1] == ONCE[1]) & (my_a >= HALF), 0.0, 1.0)
            for n in range(NB):
                bj, s = NB * cur[1] + n, n % 2
                for k in range(2):
                    elem(cur[0], bj, k, weight, masked)
                    if k == 0 and n == 0:
                        force(prev[0], NB * prev[1] + NB - 1, 1, 1)
                        host_pop(prev[0], 0)
                    else:
                        force(cur[0], bj - 1 + k, 1 - k, s if k else 1 - s)
                    if n < NB - 1:
                        issue_g(cur[0], bj + 1, k)
                    elif nxt is not None:
                        issue_g(nxt[0], NB * nxt[1], k)
                if n == 0:
                    host_pop(prev[0], 1)
                    flush(NB * prev[1] + NB - 1, 1)
                else:
                    flush(bj - 1, 1 - s)

        def start(pair):
            for k in range(2):
                issue_g(pair[0], NB * pair[1], k)

        own = (jnp.int32(0), jnp.int32(0))
        for q in range(2):
            wsc[q * 2 + 1][...] = jnp.zeros((TB, TB), BF16)
        either = jnp.where(my_t >= GT // 2, HALF, 0)

        def unit_at(n):
            v = pick([pair[1] for pair in UNITS], n)
            return pick([pair[0] for pair in UNITS], n), jnp.where(v == EITHER, either, v)

        first = unit_at(jnp.int32(0))
        start(own)
        unit(own, own, first, True)

        def two(h, carry):
            prev, cur = carry[:2], carry[2:]
            mid = unit_at(2 * h + 1)
            nxt = unit_at(jnp.minimum(2 * h + 2, len(UNITS) - 1))
            unit(prev, cur, mid, False)
            unit(cur, mid, nxt, False)
            return *mid, *nxt

        last = lax.fori_loop(0, len(UNITS) // 2, two, (*own, *first))[:2]
        force(last[0], NB * last[1] + NB - 1, 1, 1)
        for k in range(2):
            for q in range(2):
                for p in range(NP):
                    pltpu.matmul_pop(G(q, k, p))
        flush(NB * last[1] + NB - 1, 1)
        for k in range(2):
            host_pop(last[0], k)

    specs = [pltpu.ACC(q)((PR, TB), F32) for q in range(2) for k in range(2) for p in range(NP)]
    specs += [pltpu.ACC(q)((128, TB), F32) for q in range(2) for k in range(2)]
    specs += [pltpu.ACC(q)((128, TB), F32) for q in range(2) for s in range(2)]
    pl.run_scoped(run, *specs)
    total = jnp.zeros((8, TB), F32)
    for n in range(GT * NB):
        total = total + su[n]
    en[...] = total[:, :128] + total[:, 128:]
    for n in range(GT):
        finish_u(n)
    for n in range(HALF + 1):
        finish_v(n)


def solution(mesh):
    def per_device(x_own, q_own):
        rows, feat = x_own.shape
        inv_len2 = 1.0 / feat
        sq = jnp.sum(jnp.square(x_own.astype(F32)), axis=1)
        half = -jnp.minimum(0.5 * sq, 1.7e38)
        ext = [p.reshape(8, 128) for v in (half, q_own) for p in split3(v)]
        block = jnp.concatenate([x_own] + ext, axis=0)
        vm, hbm = pl.BlockSpec(memory_space=pltpu.VMEM), pl.BlockSpec(memory_space=pl.ANY)
        nu, nv, nr = GT * NB, (HALF + 1) * NB, GT + HALF
        dma = pltpu.SemaphoreType.DMA
        shape = jax.ShapeDtypeStruct
        xe = pl.pallas_call(
            gather_kernel, out_shape=shape((nr, OWN + EXT, 128), BF16), in_specs=[vm], out_specs=hbm,
            scratch_shapes=[dma(()), dma((nr,)), dma((nr,))],
            compiler_params=pltpu.CompilerParams(collective_id=0, has_side_effects=True), name='gather_blocks',
        )(block)
        place = jnp.stack(grid_of(lax.axis_index('seg'), lax.axis_index('col'))).astype(jnp.int32)
        fu, fv, en = pl.pallas_call(
            functools.partial(pair_kernel, inv_len2 * math.log2(math.e)),
            out_shape=[shape((nu, 128, TB), F32), shape((nv, 128, TB), F32), shape((8, 128), F32)],
            in_specs=[pl.BlockSpec(memory_space=pltpu.SMEM), vm],
            out_specs=[vm, vm, vm],
            scratch_shapes=[pltpu.VMEM((nu, TB, TB), BF16), pltpu.VMEM((nv, TB, TB), BF16),
                            pltpu.VMEM((nv, 128, TB), BF16), pltpu.VMEM((nu, 8, TB), F32),
                            pltpu.VMEM((nv, TB, 128), F32), pltpu.VMEM((nu, 8, TB), F32),
                            pltpu.VMEM((nv, TB, 128), F32)] + [pltpu.VMEM((TB, TB), BF16)] * 4,
            compiler_params=pltpu.CompilerParams(vmem_limit_bytes=48 * 2**20),
            name='pair_tiles',
        )(place, xe)
        force, en = pl.pallas_call(
            functools.partial(reduce_kernel, inv_len2),
            out_shape=[shape((rows, feat), F32), shape((8, 128), F32)],
            in_specs=[hbm, hbm, vm], out_specs=[vm, vm],
            scratch_shapes=[pltpu.VMEM((nr - 1, NB, 128, TB), F32), pltpu.VMEM((GT, 8, 128), F32),
                            pltpu.VMEM((GA, 8, 128), F32), pltpu.VMEM((2, NB, 128, TB), F32), dma((2,)),
                            dma((nr,)), dma((nr,)), dma((GT + GA,)), dma((GT + GA,))],
            compiler_params=pltpu.CompilerParams(collective_id=1, has_side_effects=True), name='reduce_forces',
        )(fu, fv, en)
        return force, jnp.sum(en).reshape(1)

    row_spec = P(ROW_AXES, None)

    def step(x, q):
        with jax.sharding.use_abstract_mesh(mesh.abstract_mesh):
            return jax.shard_map(per_device, mesh=mesh, in_specs=(row_spec, P(ROW_AXES)),
                                 out_specs=(row_spec, P('sys')), check_vma=False)(x, q)
    return step
```

time: 425 us -> 270 us (0.64)
  Pallas kernels: 116 us -> 258 us
  waiting for transfers between devices: 135 us -> 0 us
  blocking collectives: 75.1 us -> 0 us
  starting transfers between devices: 71.1 us -> 0 us
  local copies, waits for them, and re-layouts: 18.6 us -> 6.15 us
    pallas_call x0 -> x2, Pallas kernels: none -> 148 us  [the longest x1 111 us: per_device(): pl.pallas_call(functools.partial(reduce_kernel, inv_len2), out_shape=[sha...]
    ppermute x30 -> x0, waiting for transfers between devices: 135 us -> none  [the longest x7 42.7 us: per_device(): lax.ppermute(block, axes, shift_pairs(0, d))]
    psum x1 -> x0, blocking collectives: 75.1 us -> none  [per_device(): energy = lax.psum(jnp.sum(en), axes)]
    ppermute x30 -> x0, starting transfers between devices: 71.1 us -> none  [the longest x8 26.6 us: per_device(): lax.ppermute(fv[d], axes, shift_pairs(-d, 0))]
    unnamed x30 -> x8, local copies, waits for them, and re-layouts: 12.8 us -> 6.15 us
    pallas_call x1, Pallas kernels: 116 us -> 110 us  [per_device(): pl.pallas_call(functools.partial(pair_kernel, inv_len2 * math.log2(math.e...]
  transfers between devices with their start and end apart: 30 -> 0, of which waited for: 17 -> 0; matrix products, arithmetic and copies ran while one was open for 3% -> 0% of each run, Pallas kernels for 0% -> 0%
where the time goes in v2:
time: 270 us
  Pallas kernels  258 us (96%)
  local copies, waits for them, and re-layouts  6.15 us (2%)
  other arithmetic  4.66 us (2%)
    pallas_call x1, Pallas kernels, per_device(): pl.pallas_call(functools.partial(reduce_kernel, inv_len2), out_shape=[sha...  111 us
    pallas_call x1, Pallas kernels, per_device(): pl.pallas_call(functools.partial(pair_kernel, inv_len2 * math.log2(math.e...  110 us
    pallas_call x1, Pallas kernels, per_device(): pl.pallas_call(gather_kernel, out_shape=shape((nr, OWN + EXT, 128), BF16)...  37.8 us
    unnamed x8, local copies, waits for them, and re-layouts  6.15 us

profile of v2, /device:TPU:1, one launch (start us, length us, event | category | flops | bytes accessed | tf_op | source)
XLA Modules:
  0.0 270.0 jit_solution(11803478269008191588)
XLA Ops:
  0.7 0.1 pad_add_fusion.place
  0.8 1.2 multiply_reduce_fusion
  2.0 1.0 constant_dynamic-update-slice_fusion.6
  3.0 0.7 constant_dynamic-update-slice_fusion.2
  3.7 0.7 constant_dynamic-update-slice_fusion.1
  4.4 0.7 constant_dynamic-update-slice_fusion.blk
  5.1 0.0 copy-start.2
  5.1 0.7 copy-done.2
  5.8 37.8 %gather_blocks.1.xe = bf16[16,1072,128]{2,1,0:T(8,128)(2,1)} custom-call(bf16[1072,128]{1,0:T(8,128)(2,1)} %copy-done.2), custom_call_target="tpu_custom_call" | custom-call | tf_op jit(solution)/shard_map/gather_blocks/pallas_call | solution.py:357
  43.6 110.1 %pair_tiles.1 = (f32[32,128,256]{2,1,0:T(8,128)S(1)}, f32[36,128,256]{2,1,0:T(8,128)}, f32[8,128]{1,0:T(8,128)S(1)}) custom-call(s32[2]{0:T(128)S(1)} %pad_add_fusion.place, bf16[16,1072,128]{2,1,0:T(8,128)(2,1)} %gather_blocks.1.xe), custom_call_target="tpu_custom_call" | custom-call | tf_op jit(solution)/shard_map/pair_tiles/pallas_call | solution.py:363
  153.7 0.0 copy-start
  153.7 2.0 copy-done
  155.7 0.0 copy-start.1
  155.7 0.6 copy-done.1
  156.3 110.5 %reduce_forces.1 = (f32[1024,128]{1,0:T(8,128)}, f32[8,128]{1,0:T(8,128)}) custom-call(f32[32,128,256]{2,1,0:T(8,128)} %copy-done, f32[36,128,256]{2,1,0:T(8,128)} %get-tuple-element.8.fv, f32[8,128]{1,0:T(8,128)} %copy-done.1), custom_call_target="tpu_custom_call" | custom-call | tf_op jit(solution)/shard_map/reduce_forces/pallas_call | solution.py:375
  266.8 1.3 reduce_sum.19
  268.1 1.9 copy.11
  (3 shorter events, 0.0 us)
Async XLA Ops:
  5.1 0.7 copy-start.2
  153.7 2.0 copy-start
  155.7 0.6 copy-start.1

commit v3 on v2

--- a/solution.py
+++ b/solution.py
@@ -34,12 +34,12 @@
     z, y, x = seg // 16, (seg // 4) % 4, seg % 4
     ya = y // 2
     yb = (ya + y % 2) % 2
-    return (z * 2 + ya) * 2 + col, x * 2 + yb
+    return (col * 2 + ya) * 4 + z, x * 2 + yb
 
 
 def device_at(a, t):
-    ya, yb = (a // 2) % 2, t % 2
-    return {'seg': (a // 4) * 16 + (2 * ya + (ya + yb) % 2) * 4 + t // 2, 'col': a % 2}
+    ya, yb = (a // 4) % 2, t % 2
+    return {'seg': (a % 4) * 16 + (2 * ya + (ya + yb) % 2) * 4 + t // 2, 'col': a // 8}
 
 
 def split3(v):

time: 270 us -> 250 us (0.926); the launches traced: 270 us -> 247 us
  Pallas kernels: 258 us -> 236 us
    pallas_call x1, Pallas kernels: 111 us -> 83.5 us  [per_device(): pl.pallas_call(functools.partial(reduce_kernel, inv_len2), out_shape=[sha...]
    pallas_call x1, Pallas kernels: 37.8 us -> 42.1 us  [per_device(): pl.pallas_call(gather_kernel, out_shape=shape((nr, OWN + EXT, 128), BF16)...]
where the time goes in v3:
time: 250 us; the launch traced here: 247 us
  Pallas kernels  236 us (94%)
  local copies, waits for them, and re-layouts  6.15 us (2%)
  other arithmetic  4.66 us (2%)
    pallas_call x1, Pallas kernels, per_device(): pl.pallas_call(functools.partial(pair_kernel, inv_len2 * math.log2(math.e...  110 us
    pallas_call x1, Pallas kernels, per_device(): pl.pallas_call(functools.partial(reduce_kernel, inv_len2), out_shape=[sha...  83.5 us
    pallas_call x1, Pallas kernels, per_device(): pl.pallas_call(gather_kernel, out_shape=shape((nr, OWN + EXT, 128), BF16)...  42.1 us
    unnamed x8, local copies, waits for them, and re-layouts  6.15 us

profile of v3, /device:TPU:1, one launch (start us, length us, event | category | flops | bytes accessed | tf_op | source)
XLA Modules:
  0.0 247.2 jit_solution(16676835925421461436)
XLA Ops:
  0.7 0.1 pad_add_fusion.place
  0.8 1.2 multiply_reduce_fusion
  2.0 1.0 constant_dynamic-update-slice_fusion.6
  3.0 0.7 constant_dynamic-update-slice_fusion.2
  3.7 0.7 constant_dynamic-update-slice_fusion.1
  4.4 0.7 constant_dynamic-update-slice_fusion.blk
  5.1 0.0 copy-start.2
  5.1 0.7 copy-done.2
  5.8 42.1 %gather_blocks.1.xe = bf16[16,1072,128]{2,1,0:T(8,128)(2,1)} custom-call(bf16[1072,128]{1,0:T(8,128)(2,1)} %copy-done.2), custom_call_target="tpu_custom_call" | custom-call | tf_op jit(solution)/shard_map/gather_blocks/pallas_call | solution.py:357
  47.9 110.1 %pair_tiles.1 = (f32[32,128,256]{2,1,0:T(8,128)S(1)}, f32[36,128,256]{2,1,0:T(8,128)}, f32[8,128]{1,0:T(8,128)S(1)}) custom-call(s32[2]{0:T(128)S(1)} %pad_add_fusion.place, bf16[16,1072,128]{2,1,0:T(8,128)(2,1)} %gather_blocks.1.xe), custom_call_target="tpu_custom_call" | custom-call | tf_op jit(solution)/shard_map/pair_tiles/pallas_call | solution.py:363
  158.0 0.0 copy-start
  158.0 2.0 copy-done
  160.0 0.0 copy-start.1
  160.0 0.6 copy-done.1
  160.6 83.5 %reduce_forces.1 = (f32[1024,128]{1,0:T(8,128)}, f32[8,128]{1,0:T(8,128)}) custom-call(f32[32,128,256]{2,1,0:T(8,128)} %copy-done, f32[36,128,256]{2,1,0:T(8,128)} %get-tuple-element.8.fv, f32[8,128]{1,0:T(8,128)} %copy-done.1), custom_call_target="tpu_custom_call" | custom-call | tf_op jit(solution)/shard_map/reduce_forces/pallas_call | solution.py:375
  244.1 1.3 reduce_sum.19
  245.4 1.9 copy.11
  (3 shorter events, 0.0 us)
Async XLA Ops:
  5.1 0.7 copy-start.2
  158.0 2.0 copy-start
  160.0 0.6 copy-start.1

commit v4 on v3

--- a/solution.py
+++ b/solution.py
@@ -15,17 +15,17 @@
 OWN = 1024
 TB = 256
 NB = OWN // TB
+LANES, SUB, NEXT = 128, 8, 2
 EXT = 48
 PR = 64
 NP = TB // PR
 HALF = GA // 2
-HOST_STEP = (0, 1, 7, 4, 3, 5, 6, 2)
 EITHER = -1
 MESH = pl.DeviceIdType.MESH
 
 UNITS = [(u, v) for u in range(GT) for v in range(1, HALF)]
-UNITS += [(HOST_STEP.index(d), v) for d in (1, 2, 3) for v in (0, HALF)]
-UNITS += [(HOST_STEP.index(4), EITHER), (0, HALF)]
+UNITS += [(u, v) for u in (1, 2, 3) for v in (0, HALF)]
+UNITS += [(4, EITHER), (0, HALF)]
 UNITS.sort(key=lambda pair: pair[0])
 ONCE = (0, HALF)
 
@@ -40,13 +40,6 @@
 def device_at(a, t):
     ya, yb = (a // 4) % 2, t % 2
     return {'seg': (a % 4) * 16 + (2 * ya + (ya + yb) % 2) * 4 + t // 2, 'col': a // 8}
-
-
-def split3(v):
-    hi = lax.reduce_precision(v, 8, 7)
-    mid = lax.reduce_precision(v - hi, 8, 7)
-    lo = lax.reduce_precision(v - hi - mid, 8, 7)
-    return [p.astype(BF16) for p in (hi, mid, lo)]
 
 
 def pick(table, n):
@@ -60,6 +53,7 @@
 class Ring:
     def __init__(self):
         self.a, self.t = grid_of(lax.axis_index('seg'), lax.axis_index('col'))
+        self.flip = 1 - 2 * (self.t % 2)
 
     def peer(self, da, dt):
         return device_at((self.a + da + GA) % GA, (self.t + dt + GT) % GT)
@@ -73,49 +67,102 @@
         pl.semaphore_wait(barrier, GT + GA - 2)
 
 
-def gather_kernel(blk, xe, own, snd, rcv):
+def split3(v):
+    parts = []
+    for _ in range(3):
+        parts.append(v.astype(BF16))
+        v = v - parts[-1].astype(F32)
+    return parts
+
+
+def gather_kernel(x, q, xe, blk, half, own, snd, rcv):
     ring = Ring()
+    flip = ring.flip
+    blk[0:OWN, :] = x[...]
+    for r in range(OWN // LANES):
+        rows = x[r * LANES:(r + 1) * LANES, :].astype(F32)
+        half[r:r + 1, :] = jnp.sum((rows * rows).T, axis=0, keepdims=True)
+    for n, part in enumerate(split3(-jnp.minimum(0.5 * half[...], 1.7e38)) + split3(q[...])):
+        blk[OWN + SUB * n:OWN + SUB * (n + 1), :] = part
+
+    def slot_u(dx):
+        return (2 * dx + flip + GT) % GT
+
+    def slot_v(d):
+        return GT - 1 + d
+
+    copies = []
+
+    def copy(src, slot, a=0, t=0):
+        m = len(copies)
+        copies.append(pltpu.make_async_remote_copy(src_ref=src, dst_ref=xe.at[slot], send_sem=snd.at[m], recv_sem=rcv.at[m],
+                                                   device_id=ring.peer(a, t), device_id_type=MESH))
+        return copies[-1]
+
+    right, left = -NEXT % GT, NEXT
+    own_right, own_left = copy(blk, right, t=NEXT), copy(blk, left, t=-NEXT)
+    own_over = copy(blk, (GT - flip) % GT, t=flip)
+    pass_right = copy(xe.at[right], 2 * NEXT, t=NEXT)
+    over = xe.at[slot_u(0)]
+    over_right, over_left = copy(over, slot_u(-1), t=NEXT), copy(over, slot_u(1), t=-NEXT)
+    over_pass = copy(xe.at[slot_u(1)], slot_u(2), t=-NEXT)
+    direct = {d: copy(blk, slot_v(d), a=-d) for d in range(1, HALF + 1) if d % 4 != 2}
+    pass_down = copy(xe.at[slot_v(1)], slot_v(2), a=-1)
+    pass_up = copy(xe.at[slot_v(7)], slot_v(6), a=1)
+    ring.enter()
     keep = pltpu.make_async_copy(blk, xe.at[0], own)
     keep.start()
-    ring.enter()
+    for c in (own_over, own_right, own_left, direct[1], direct[7], direct[4], direct[3], direct[5], direct[8]):
+        c.start()
+    through = ((own_over, (over_right, over_left)), (own_right, (pass_right,)), (direct[1], (pass_down,)),
+               (direct[7], (pass_up,)), (over_left, (over_pass,)))
+    for got, then in through:
+        got.wait_recv()
+        for c in then:
+            c.start()
+    for c in copies:
+        if all(c is not got for got, _ in through):
+            c.wait_recv()
+    for c in copies:
+        c.wait_send()
+    keep.wait()
+
+
+def reduce_kernel(inv_len2, fu, fv, en, force_out, en_out, rb, er, ec, fsnd, frcv, esnd, ercv):
+    ring = Ring()
+    flip = ring.flip
+
+    def same(dx):
+        return pl.multiple_of(NB * ((2 * dx + GT) % GT), NB)
+
+    def other(dx):
+        return pl.multiple_of(NB * ((2 * dx + flip + GT) % GT), NB)
+
     copies = []
-    for n in range(1, HALF + 1):
-        for slot in ([GT - 1 + n, n] if n < GT else [GT - 1 + n]):
-            to = ring.peer(0, -HOST_STEP[slot]) if slot < GT else ring.peer(-(slot - GT + 1), 0)
-            copies.append(pltpu.make_async_remote_copy(src_ref=blk, dst_ref=xe.at[slot], send_sem=snd.at[slot],
-                                                       recv_sem=rcv.at[slot], device_id=to, device_id_type=MESH))
-            copies[-1].start()
-    keep.wait()
-    for copy in copies:
-        copy.wait_recv()
-    for copy in copies:
-        copy.wait_send()
-
-
-def reduce_kernel(inv_len2, fu, fv, en, force_out, en_out, rb, er, ec, mine, own, fsnd, frcv, esnd, ercv):
-    ring = Ring()
-    keep = [pltpu.make_async_copy(f.at[pl.ds(0, NB)], mine.at[n], own.at[n]) for n, f in enumerate((fu, fv))]
-    for copy in keep:
-        copy.start()
-    ring.enter()
-    copies = []
-    for n in range(1, HALF + 1):
-        for slot in ([GT - 1 + n, n] if n < GT else [GT - 1 + n]):
-            src = fu.at[pl.ds(NB * slot, NB)] if slot < GT else fv.at[pl.ds(NB * (slot - GT + 1), NB)]
-            to = ring.peer(0, HOST_STEP[slot]) if slot < GT else ring.peer(slot - GT + 1, 0)
-            copies.append(pltpu.make_async_remote_copy(src_ref=src, dst_ref=rb.at[slot - 1], send_sem=fsnd.at[slot],
-                                                       recv_sem=frcv.at[slot], device_id=to, device_id_type=MESH))
-            copies[-1].start()
+
+    def copy(src, first, a=0, t=0):
+        m = len(copies)
+        src = src if first is None else src.at[pl.ds(first, NB)]
+        copies.append(pltpu.make_async_remote_copy(src_ref=src, dst_ref=rb.at[m], send_sem=fsnd.at[m], recv_sem=frcv.at[m],
+                                                   device_id=ring.peer(a, t), device_id_type=MESH))
+        return m
+
+    far_o, far_s = copy(fu, other(2), t=-NEXT), copy(fu, same(2), t=NEXT)
+    near_o, near_s = copy(fu, other(1), t=NEXT), copy(fu, same(-1), t=-NEXT)
+    sum_o, sum_s = copy(rb.at[far_o], None, t=-NEXT), copy(rb.at[far_s], None, t=NEXT)
+    over = copy(rb.at[near_o], None, t=flip)
+    up, down = copy(fv, NB * 2, a=1), copy(fv, NB * 6, a=-1)
+    direct = [copy(fv, NB * d, a=d) for d in (4, 3, 5, 8)]
+    sum_up, sum_down = copy(rb.at[up], None, a=1), copy(rb.at[down], None, a=7)
 
     def spread(ref, me, along_t):
         out = []
         for n in range(1, GT if along_t else GA):
             k = n if along_t else GT + n
-            out.append(pltpu.make_async_remote_copy(src_ref=ref.at[me], dst_ref=ref.at[me], send_sem=esnd.at[k],
-                                                    recv_sem=ercv.at[k], device_id=ring.peer(0, n) if along_t else ring.peer(n, 0),
-                                                    device_id_type=MESH))
-        for copy in out:
-            copy.start()
+            out.append(pltpu.make_async_remote_copy(src_ref=ref.at[me], dst_ref=ref.at[me], send_sem=esnd.at[k], recv_sem=ercv.at[k],
+                                                    device_id=ring.peer(*((0, n) if along_t else (n, 0))), device_id_type=MESH))
+        for c in out:
+            c.start()
         return out
 
     def fold(r, count):
@@ -124,30 +171,55 @@
             total = total + r[n]
         return total
 
+    def add(m, ref, first):
+        copies[m].wait_recv()
+
+        def one(ib, _):
+            rb[m, ib] = rb[m, ib] + ref[first + ib]
+            return 0
+        lax.fori_loop(0, NB, one, 0)
+
     er[ring.t] = en[...]
-    for copy in keep:
-        copy.wait()
+    ring.enter()
+    for m in (far_o, up, down, far_s, near_o, direct[0], near_s, *direct[1:]):
+        copies[m].start()
     along = spread(er, ring.t, True)
-    for copy in along:
-        copy.wait_recv()
+    for c in along:
+        c.wait_recv()
     ec[ring.a] = fold(er, GT)
-    copies[0].wait_recv()
+    add(far_o, fu, other(-1))
+    add(up, fv, NB)
+    copies[sum_o].start()
+    add(down, fv, NB * 7)
+    copies[sum_up].start()
+    add(far_s, fu, same(1))
+    copies[sum_down].start()
     across = spread(ec, ring.a, False)
-    for copy in copies[1:]:
-        copy.wait_recv()
-    for copy in across:
-        copy.wait_recv()
-    en_out[...] = fold(ec, GA)
+    copies[sum_s].start()
+    copies[sum_o].wait_recv()
+    copies[near_o].wait_recv()
+
+    def beside(ib, _):
+        rb[near_o, ib] = rb[near_o, ib] + rb[sum_o, ib] + fu[other(0) + ib]
+        return 0
+    lax.fori_loop(0, NB, beside, 0)
+    for c in across:
+        c.wait_recv()
+    en_out[0] = jnp.sum(fold(ec, GA))
+    copies[over].start()
+    late = (near_s, sum_s, *direct, sum_up, sum_down, over)
+    for m in late:
+        copies[m].wait_recv()
 
     def all_sum(ib, _):
-        out = mine[0, ib] + mine[1, ib]
-        for slot in range(GT + HALF - 1):
-            out = out + rb[slot, ib]
+        out = fu[ib] + fv[ib]
+        for m in late:
+            out = out + rb[m, ib]
         force_out[pl.ds(pl.multiple_of(ib * TB, TB), TB), :] = (out * inv_len2).T
         return 0
     lax.fori_loop(0, NB, all_sum, 0)
-    for copy in copies + along + across:
-        copy.wait_send()
+    for c in [*copies, *along, *across]:
+        c.wait_send()
 
 
 def pair_kernel(scale, place, xe, fu, fv, en, xi, xv, xtv, qu, qv, su, sv, *wsc):
@@ -346,19 +418,15 @@
     def per_device(x_own, q_own):
         rows, feat = x_own.shape
         inv_len2 = 1.0 / feat
-        sq = jnp.sum(jnp.square(x_own.astype(F32)), axis=1)
-        half = -jnp.minimum(0.5 * sq, 1.7e38)
-        ext = [p.reshape(8, 128) for v in (half, q_own) for p in split3(v)]
-        block = jnp.concatenate([x_own] + ext, axis=0)
         vm, hbm = pl.BlockSpec(memory_space=pltpu.VMEM), pl.BlockSpec(memory_space=pl.ANY)
         nu, nv, nr = GT * NB, (HALF + 1) * NB, GT + HALF
         dma = pltpu.SemaphoreType.DMA
         shape = jax.ShapeDtypeStruct
         xe = pl.pallas_call(
-            gather_kernel, out_shape=shape((nr, OWN + EXT, 128), BF16), in_specs=[vm], out_specs=hbm,
-            scratch_shapes=[dma(()), dma((nr,)), dma((nr,))],
+            gather_kernel, out_shape=shape((nr, OWN + EXT, 128), BF16), in_specs=[vm, vm], out_specs=hbm,
+            scratch_shapes=[pltpu.VMEM((OWN + EXT, LANES), BF16), pltpu.VMEM((SUB, LANES), F32), dma(()), dma((nr,)), dma((nr,))],
             compiler_params=pltpu.CompilerParams(collective_id=0, has_side_effects=True), name='gather_blocks',
-        )(block)
+        )(x_own, q_own.reshape(SUB, LANES))
         place = jnp.stack(grid_of(lax.axis_index('seg'), lax.axis_index('col'))).astype(jnp.int32)
         fu, fv, en = pl.pallas_call(
             functools.partial(pair_kernel, inv_len2 * math.log2(math.e)),
@@ -374,14 +442,13 @@
         )(place, xe)
         force, en = pl.pallas_call(
             functools.partial(reduce_kernel, inv_len2),
-            out_shape=[shape((rows, feat), F32), shape((8, 128), F32)],
-            in_specs=[hbm, hbm, vm], out_specs=[vm, vm],
+            out_shape=[shape((rows, feat), F32), shape((1,), F32)],
+            in_specs=[vm, vm, vm], out_specs=[vm, pl.BlockSpec(memory_space=pltpu.SMEM)],
             scratch_shapes=[pltpu.VMEM((nr - 1, NB, 128, TB), F32), pltpu.VMEM((GT, 8, 128), F32),
-                            pltpu.VMEM((GA, 8, 128), F32), pltpu.VMEM((2, NB, 128, TB), F32), dma((2,)),
-                            dma((nr,)), dma((nr,)), dma((GT + GA,)), dma((GT + GA,))],
-            compiler_params=pltpu.CompilerParams(collective_id=1, has_side_effects=True), name='reduce_forces',
+                            pltpu.VMEM((GA, 8, 128), F32), dma((nr,)), dma((nr,)), dma((GT + GA,)), dma((GT + GA,))],
+            compiler_params=pltpu.CompilerParams(vmem_limit_bytes=32 * 2**20, collective_id=1, has_side_effects=True), name='reduce_forces',
         )(fu, fv, en)
-        return force, jnp.sum(en).reshape(1)
+        return force, en
 
     row_spec = P(ROW_AXES, None)
 

time: 250 us -> 218 us (0.87); the launches traced: 247 us -> 218 us
  Pallas kernels: 236 us -> 212 us
  other arithmetic: 4.66 us -> 0.08 us
  local copies, waits for them, and re-layouts: 6.15 us -> 3.13 us
    pallas_call x1, Pallas kernels: 83.5 us -> 65.9 us  [per_device(): pl.pallas_call(functools.partial(reduce_kernel, inv_len2), out_shape=[sha...]
    pallas_call x1, Pallas kernels: 42.1 us -> 36.2 us  [per_device(): pl.pallas_call(gather_kernel, out_shape=shape((nr, OWN + EXT, 128), BF16)...]
    unnamed x8 -> x3, local copies, waits for them, and re-layouts: 6.15 us -> 3.13 us
where the time goes in v4:
time: 218 us
  Pallas kernels  212 us (97%)
  local copies, waits for them, and re-layouts  3.13 us (1%)
  between operations  2.5 us (1%)
    pallas_call x1, Pallas kernels, per_device(): pl.pallas_call(functools.partial(pair_kernel, inv_len2 * math.log2(math.e...  110 us
    pallas_call x1, Pallas kernels, per_device(): pl.pallas_call(functools.partial(reduce_kernel, inv_len2), out_shape=[sha...  65.9 us
    pallas_call x1, Pallas kernels, per_device(): pl.pallas_call(gather_kernel, out_shape=shape((nr, OWN + EXT, 128), BF16)...  36.2 us

profile of v4, /device:TPU:1, one launch (start us, length us, event | category | flops | bytes accessed | tf_op | source)
XLA Modules:
  0.0 217.9 jit_solution(1090735353478580464)
XLA Ops:
  0.7 0.1 pad_add_fusion.place
  0.8 36.2 %gather_blocks.1.xe = bf16[16,1072,128]{2,1,0:T(8,128)(2,1)} custom-call(bf16[1024,128]{1,0:T(8,128)(2,1)} %x.1, f32[8,128]{1,0:T(8,128)} %bitcast.3), custom_call_target="tpu_custom_call" | custom-call | tf_op jit(solution)/shard_map/gather_blocks/pallas_call | solution.py:425
  37.0 110.1 %pair_tiles.1 = (f32[32,128,256]{2,1,0:T(8,128)S(1)}, f32[36,128,256]{2,1,0:T(8,128)}, f32[8,128]{1,0:T(8,128)S(1)}) custom-call(s32[2]{0:T(128)S(1)} %pad_add_fusion.place, bf16[16,1072,128]{2,1,0:T(8,128)(2,1)} %gather_blocks.1.xe), custom_call_target="tpu_custom_call" | custom-call | tf_op jit(solution)/shard_map/pair_tiles/pallas_call | solution.py:431
  147.1 0.0 copy-start
  147.1 2.3 %copy-done = f32[36,128,256]{2,1,0:T(8,128)S(1)} copy-done((f32[36,128,256]{2,1,0:T(8,128)S(1)}, f32[36,128,256]{2,1,0:T(8,128)}, u32[]{:S(2)}) %copy-start) | copy-done | bytes 4718616
  149.5 65.9 %reduce_forces.1 = (f32[1024,128]{1,0:T(8,128)S(1)}, f32[1]{0:T(128)}) custom-call(f32[32,128,256]{2,1,0:T(8,128)S(1)} %get-tuple-element.5.fu, f32[36,128,256]{2,1,0:T(8,128)S(1)} %copy-done, f32[8,128]{1,0:T(8,128)S(1)} %get-tuple-element.7.en), custom_call_target="tpu_custom_call" | custom-call | tf_op jit(solution)/shard_map/reduce_forces/pallas_call | solution.py:443
  215.4 0.8 copy.6
Async XLA Ops:
  147.1 2.3 %copy-start = (f32[36,128,256]{2,1,0:T(8,128)S(1)}, f32[36,128,256]{2,1,0:T(8,128)}, u32[]{:S(2)}) copy-start(f32[36,128,256]{2,1,0:T(8,128)} %get-tuple-element.6.fv) | copy-start | bytes 14155780

commit v5 on v4

--- a/solution.py
+++ b/solution.py
@@ -75,7 +75,7 @@
     return parts
 
 
-def gather_kernel(x, q, xe, blk, half, own, snd, rcv):
+def gather_kernel(x, q, xe, blk, half, snd, rcv):
     ring = Ring()
     flip = ring.flip
     blk[0:OWN, :] = x[...]
@@ -110,8 +110,6 @@
     pass_down = copy(xe.at[slot_v(1)], slot_v(2), a=-1)
     pass_up = copy(xe.at[slot_v(7)], slot_v(6), a=1)
     ring.enter()
-    keep = pltpu.make_async_copy(blk, xe.at[0], own)
-    keep.start()
     for c in (own_over, own_right, own_left, direct[1], direct[7], direct[4], direct[3], direct[5], direct[8]):
         c.start()
     through = ((own_over, (over_right, over_left)), (own_right, (pass_right,)), (direct[1], (pass_down,)),
@@ -123,9 +121,9 @@
     for c in copies:
         if all(c is not got for got, _ in through):
             c.wait_recv()
+    xe[0] = blk[...]
     for c in copies:
         c.wait_send()
-    keep.wait()
 
 
 def reduce_kernel(inv_len2, fu, fv, en, force_out, en_out, rb, er, ec, fsnd, frcv, esnd, ercv):
@@ -181,15 +179,16 @@
 
     er[ring.t] = en[...]
     ring.enter()
-    for m in (far_o, up, down, far_s, near_o, direct[0], near_s, *direct[1:]):
+    for m in (far_o, up, down, far_s, near_o, *direct):
         copies[m].start()
     along = spread(er, ring.t, True)
+    add(far_o, fu, other(-1))
     for c in along:
         c.wait_recv()
     ec[ring.a] = fold(er, GT)
-    add(far_o, fu, other(-1))
+    copies[sum_o].start()
+    copies[near_s].start()
     add(up, fv, NB)
-    copies[sum_o].start()
     add(down, fv, NB * 7)
     copies[sum_up].start()
     add(far_s, fu, same(1))
@@ -418,14 +417,14 @@
     def per_device(x_own, q_own):
         rows, feat = x_own.shape
         inv_len2 = 1.0 / feat
-        vm, hbm = pl.BlockSpec(memory_space=pltpu.VMEM), pl.BlockSpec(memory_space=pl.ANY)
+        vm = pl.BlockSpec(memory_space=pltpu.VMEM)
         nu, nv, nr = GT * NB, (HALF + 1) * NB, GT + HALF
         dma = pltpu.SemaphoreType.DMA
         shape = jax.ShapeDtypeStruct
         xe = pl.pallas_call(
-            gather_kernel, out_shape=shape((nr, OWN + EXT, 128), BF16), in_specs=[vm, vm], out_specs=hbm,
-            scratch_shapes=[pltpu.VMEM((OWN + EXT, LANES), BF16), pltpu.VMEM((SUB, LANES), F32), dma(()), dma((nr,)), dma((nr,))],
-            compiler_params=pltpu.CompilerParams(collective_id=0, has_side_effects=True), name='gather_blocks',
+            gather_kernel, out_shape=shape((nr, OWN + EXT, 128), BF16), in_specs=[vm, vm], out_specs=vm,
+            scratch_shapes=[pltpu.VMEM((OWN + EXT, LANES), BF16), pltpu.VMEM((SUB, LANES), F32), dma((nr,)), dma((nr,))],
+            compiler_params=pltpu.CompilerParams(vmem_limit_bytes=12 * 2**20, collective_id=0, has_side_effects=True), name='gather_blocks',
         )(x_own, q_own.reshape(SUB, LANES))
         place = jnp.stack(grid_of(lax.axis_index('seg'), lax.axis_index('col'))).astype(jnp.int32)
         fu, fv, en = pl.pallas_call(
@@ -437,7 +436,7 @@
                             pltpu.VMEM((nv, 128, TB), BF16), pltpu.VMEM((nu, 8, TB), F32),
                             pltpu.VMEM((nv, TB, 128), F32), pltpu.VMEM((nu, 8, TB), F32),
                             pltpu.VMEM((nv, TB, 128), F32)] + [pltpu.VMEM((TB, TB), BF16)] * 4,
-            compiler_params=pltpu.CompilerParams(vmem_limit_bytes=48 * 2**20),
+            compiler_params=pltpu.CompilerParams(vmem_limit_bytes=38 * 2**20),
             name='pair_tiles',
         )(place, xe)
         force, en = pl.pallas_call(
@@ -446,7 +445,7 @@
             in_specs=[vm, vm, vm], out_specs=[vm, pl.BlockSpec(memory_space=pltpu.SMEM)],
             scratch_shapes=[pltpu.VMEM((nr - 1, NB, 128, TB), F32), pltpu.VMEM((GT, 8, 128), F32),
                             pltpu.VMEM((GA, 8, 128), F32), dma((nr,)), dma((nr,)), dma((GT + GA,)), dma((GT + GA,))],
-            compiler_params=pltpu.CompilerParams(vmem_limit_bytes=32 * 2**20, collective_id=1, has_side_effects=True), name='reduce_forces',
+            compiler_params=pltpu.CompilerParams(vmem_limit_bytes=20 * 2**20, collective_id=1, has_side_effects=True), name='reduce_forces',
         )(fu, fv, en)
         return force, en
 

time: 218 us -> 215 us (0.986)
  no operation moved by 1% of the time
where the time goes in v5:
time: 215 us
  Pallas kernels  210 us (98%)
  between operations  2.48 us (1%)
  local copies, waits for them, and re-layouts  2.43 us (1%)
    pallas_call x1, Pallas kernels, per_device(): pl.pallas_call(functools.partial(pair_kernel, inv_len2 * math.log2(math.e...  108 us
    pallas_call x1, Pallas kernels, per_device(): pl.pallas_call(functools.partial(reduce_kernel, inv_len2), out_shape=[sha...  66.4 us
    pallas_call x1, Pallas kernels, per_device(): pl.pallas_call(gather_kernel, out_shape=shape((nr, OWN + EXT, 128), BF16)...  35.4 us

profile of v5, /device:TPU:1, one launch (start us, length us, event | category | flops | bytes accessed | tf_op | source)
XLA Modules:
  0.0 214.9 jit_solution(4462065239722462110)
XLA Ops:
  0.7 0.1 pad_add_fusion.place
  0.8 0.0 copy-start
  0.8 0.9 copy-done
  1.7 0.0 copy-start.1
  1.7 0.7 copy-done.1
  2.4 35.4 %gather_blocks.1.xe = bf16[16,1072,128]{2,1,0:T(8,128)(2,1)S(1)} custom-call(bf16[1024,128]{1,0:T(8,128)(2,1)S(1)} %copy-done, f32[8,128]{1,0:T(8,128)S(1)} %bitcast.3), custom_call_target="tpu_custom_call" | custom-call | tf_op jit(solution)/shard_map/gather_blocks/pallas_call | solution.py:424
  37.8 108.2 %pair_tiles.1 = (f32[32,128,256]{2,1,0:T(8,128)S(1)}, f32[36,128,256]{2,1,0:T(8,128)S(1)}, f32[8,128]{1,0:T(8,128)S(1)}) custom-call(s32[2]{0:T(128)S(1)} %pad_add_fusion.place, bf16[16,1072,128]{2,1,0:T(8,128)(2,1)S(1)} %gather_blocks.1.xe), custom_call_target="tpu_custom_call" | custom-call | tf_op jit(solution)/shard_map/pair_tiles/pallas_call | solution.py:430
  146.0 66.4 %reduce_forces.1 = (f32[1024,128]{1,0:T(8,128)S(1)}, f32[1]{0:T(128)}) custom-call(f32[32,128,256]{2,1,0:T(8,128)S(1)} %get-tuple-element.5.fu, f32[36,128,256]{2,1,0:T(8,128)S(1)} %get-tuple-element.6.fv, f32[8,128]{1,0:T(8,128)S(1)} %get-tuple-element.7.en), custom_call_target="tpu_custom_call" | custom-call | tf_op jit(solution)/shard_map/reduce_forces/pallas_call | solution.py:442
  212.4 0.8 copy.6
Async XLA Ops:
  0.8 1.0 copy-start
  1.7 0.7 copy-start.1
